TPU v7x, 768 devices: a whole 4x8x12 slice. The times are simulated.
768 devices in a mesh: dp: 24 (over z, y_lo), group: 32 (over x, y_hi, core).
Axes of the slice: x: 4, y: 8 (y_hi: 4, y_lo: 2; y = y_hi * 2 + y_lo), z: 12, core: 2. Of those that a mesh axis runs over, the one named last changes fastest.
Arguments:
- query: bfloat16 [98304, 4096], P(('dp', 'group')), may hold values from -6 to 6
- comp_key: bfloat16 [98304, 512], P(('dp', 'group')), may hold values from -6 to 6
- comp_value: bfloat16 [98304, 512], P(('dp', 'group')), may hold values from -6 to 6
- prompt_key: bfloat16 [3072, 512], P(('dp', 'group')), may hold values from -6 to 6
- prompt_value: bfloat16 [3072, 512], P(('dp', 'group')), may hold values from -6 to 6
- d_out: bfloat16 [98304, 4096], P(('dp', 'group')), may hold values from -6 to 6
- q_gain: float32 [128], replicated, may hold values from 0.5 to 1.5
- k_gain: float32 [128], replicated, may hold values from 0.5 to 1.5
- lengths: int32 [768], P(('dp', 'group')), may hold values from 1 to 128, 61440 in all
Outputs:
- d_query: bfloat16 [98304, 4096], P(('dp', 'group'))
- d_comp_key: bfloat16 [98304, 512], P(('dp', 'group'))
- d_comp_value: bfloat16 [98304, 512], P(('dp', 'group'))
- d_prompt_key: bfloat16 [3072, 512], P(('dp', 'group'))
- d_prompt_value: bfloat16 [3072, 512], P(('dp', 'group'))
- d_q_gain: float32 [128], replicated
- d_k_gain: float32 [128], replicated
Inputs may be any that keep to these rules, and one draw needn't show every extreme that they name: `lengths`: each entry is the live slots of one completion, at most 128; some completion has exactly 128.
All inputs are finite; a program needn't handle non-finite values. No bound on the sum of `lengths` on one device may be relied on, other than what follows from the above.
Results may differ from a plain program's by a relative error of at most 0.025.
Values may be sent and summed in bfloat16 or wider, within the bound.
No kernel may reach another device: no remote copies, remote signals or barrier semaphores. Data moves between devices by JAX's collectives and lax.ppermute only.
A program may use at most 64 MiB of HBM per device.

v0:
```python
import functools

import jax
import jax.numpy as jnp
from jax import lax
from jax.sharding import Mesh
from jax.sharding import PartitionSpec as P

HD = 128
HQ = 32
HK = 4
GROUP = ("group_0", "group_1", "group_2")
DP_GROUP = ("dp_0", "dp_1", "group_0", "group_1", "group_2")


EPS = 1e-06


def side_by_side(arrays, axis, dim, along):
    ends, at = ([], 0)
    for a in arrays[:-1]:
        at += a.shape[along]
        ends.append(at)
    both = jnp.concatenate(arrays, axis=along)
    return tuple(jnp.split(lax.all_gather(both, axis, axis=dim, tiled=True), ends, axis=along))


def split_up(x, dim, peers):
    shape = x.shape
    blocks = x.reshape(*shape[:dim], peers, shape[dim] // peers, *shape[dim + 1 :])
    return jnp.moveaxis(blocks, dim, 0)


def sent_and_summed(x, axis, dim):
    blocks = split_up(x, dim, lax.axis_size(axis))
    arrived = lax.all_to_all(blocks, axis, split_axis=0, concat_axis=0, tiled=True)
    return arrived.astype(jnp.float32).sum(axis=0)


def by_axis(x, axes):
    return functools.reduce(lax.psum, axes, x)


def normalize(vectors, gain):
    wide = vectors.astype(jnp.float32)
    inverse = lax.rsqrt(jnp.mean(wide * wide, axis=-1, keepdims=True) + EPS)
    unit = wide * inverse
    return ((unit * gain).astype(jnp.bfloat16), unit, inverse)


def norm_back(grad, unit, inverse, gain):
    scaled = grad * gain
    back = inverse * (scaled - unit * jnp.mean(scaled * unit, axis=-1, keepdims=True))
    return (back, jnp.sum((grad * unit).reshape(-1, unit.shape[-1]), axis=0))


def head_grads(query_head, key_head, value_head, grad_head, visible, scale):
    scores = (
        jnp.einsum("cgd,kd->gck", query_head, key_head, preferred_element_type=jnp.float32) * scale
    )
    expo = jnp.where(visible[None], jnp.exp(scores), 0.0)
    totals = jnp.sum(expo, axis=-1, keepdims=True)
    rounded = (expo / totals).astype(jnp.bfloat16)
    output = jnp.einsum("gck,kd->cgd", rounded, value_head, preferred_element_type=jnp.float32)
    delta = jnp.transpose(jnp.sum(grad_head.astype(jnp.float32) * output, axis=-1))[..., None]
    dprob = jnp.einsum("cgd,kd->gck", grad_head, value_head, preferred_element_type=jnp.float32)
    dscore = (expo / totals * (dprob - delta)).astype(jnp.bfloat16)
    dquery = jnp.einsum("gck,kd->cgd", dscore, key_head, preferred_element_type=jnp.float32) * scale
    dkey = jnp.einsum("gck,cgd->kd", dscore, query_head, preferred_element_type=jnp.float32) * scale
    dvalue = jnp.einsum("gck,cgd->kd", rounded, grad_head, preferred_element_type=jnp.float32)
    return (dquery, dkey, dvalue, totals, delta)


def local(query, comp_key, comp_value, prompt_key, prompt_value, d_out, q_gain, k_gain, lengths):
    count = query.shape[0]
    shard = prompt_key.shape[0]
    groups = HQ // HK
    scale = HD ** (-0.5)
    qnorm, qunit, qinv = normalize(query.reshape(count, HQ, HD), q_gain)
    cnorm, cunit, cinv = normalize(comp_key.reshape(count, HK, HD), k_gain)
    pnorm, punit, pinv = normalize(prompt_key.reshape(shard, HK, HD), k_gain)
    pkeys, pvalues = side_by_side((pnorm.reshape(shard, HK * HD), prompt_value), GROUP, 0, 1)
    prompt_len = pkeys.shape[0]
    keys = jnp.concatenate([pkeys, cnorm.reshape(count, HK * HD)], axis=0).reshape(-1, HK, HD)
    values = jnp.concatenate([pvalues, comp_value], axis=0).reshape(-1, HK, HD)
    slots = lax.broadcasted_iota(jnp.int32, (count, count), 0)
    others = lax.broadcasted_iota(jnp.int32, (count, count), 1)
    visible = jnp.concatenate([jnp.ones((count, prompt_len), bool), others <= slots], axis=1)
    live = (jnp.arange(count, dtype=jnp.int32) < lengths[0])[:, None]
    masked = jnp.where(live, d_out, jnp.zeros_like(d_out))
    query_four = qnorm.reshape(count, HK, groups, HD)
    grad_four = masked.reshape(count, HK, groups, HD)
    results = [
        head_grads(
            query_four[:, head], keys[:, head], values[:, head], grad_four[:, head], visible, scale
        )
        for head in range(HK)
    ]
    dquery = jnp.stack([item[0] for item in results], axis=1).reshape(count, HQ, HD)
    dkey_all = jnp.stack([item[1] for item in results], axis=1)
    dvalue_all = jnp.stack([item[2] for item in results], axis=1)
    term = jnp.concatenate(
        [
            dkey_all[:prompt_len].reshape(prompt_len, HK * HD),
            dvalue_all[:prompt_len].reshape(prompt_len, HK * HD),
        ],
        axis=1,
    )
    summed = sent_and_summed(term.astype(jnp.bfloat16), GROUP, 0)
    dkey_comp = dkey_all[prompt_len:]
    dvalue_comp = dvalue_all[prompt_len:]
    dkey_prompt = summed[:, : HK * HD].reshape(shard, HK, HD)
    dvalue_prompt = summed[:, HK * HD :]
    dq, gain_query = norm_back(dquery, qunit, qinv, q_gain)
    dck, gain_comp = norm_back(dkey_comp, cunit, cinv, k_gain)
    dpk, gain_prompt = norm_back(dkey_prompt, punit, pinv, k_gain)
    gain_query, gain_key = (
        by_axis(gain_query, DP_GROUP),
        by_axis(gain_comp + gain_prompt, DP_GROUP),
    )
    return (
        dq.reshape(count, HQ * HD).astype(jnp.bfloat16),
        dck.reshape(count, HK * HD).astype(jnp.bfloat16),
        dvalue_comp.reshape(count, HK * HD).astype(jnp.bfloat16),
        dpk.reshape(shard, HK * HD).astype(jnp.bfloat16),
        dvalue_prompt.astype(jnp.bfloat16),
        gain_query,
        gain_key,
    )


def solution(mesh):
    finer = Mesh(
        mesh.devices.reshape(12, 2, 4, 4, 2), ("dp_0", "dp_1", "group_0", "group_1", "group_2")
    )
    placed = (
        P(DP_GROUP, None),
        P(DP_GROUP, None),
        P(DP_GROUP, None),
        P(DP_GROUP, None),
        P(DP_GROUP, None),
        P(DP_GROUP, None),
        P(),
        P(),
        P(DP_GROUP),
    )
    return jax.shard_map(
        local,
        mesh=finer,
        in_specs=placed,
        out_specs=(
            P(DP_GROUP, None),
            P(DP_GROUP, None),
            P(DP_GROUP, None),
            P(DP_GROUP, None),
            P(DP_GROUP, None),
            P(),
            P(),
        ),
        check_vma=False,
    )
```

profile of v0, /device:TPU:1, one launch (start us, length us, event | category | flops | bytes accessed | tf_op | source)
XLA Modules:
  0.0 206.5 jit_solution(3982246941759269518)
XLA Ops:
  2.8 1.0 copy.252
  5.6 49.8 %all-gather = bf16[32,4,1024]{2,1,0:T(4,128)(2,1)S(1)} all-gather(bf16[1,4,1024]{2,1,0:T(4,128)(2,1)S(1)} %maximum_bitcast_fusion), channel_id=1, replica_groups=mesh['dp_0'=12,'dp_1'=2,'group_0'=4,'group_1'=4,'group_2'=2] {'group_0',..., dimensions={0}, use_global_device_ids=true | all-gather | bytes 270336 | tf_op jit(solution)/shard_map/all_gather | solution.py:25
  58.5 1.3 concatenate.30
  60.5 2.1 %multiply_convert_fusion = bf16[128,4,8,128]{3,0,2,1:T(8,128)(2,1)} fusion(f32[128,4,8,128]{3,0,2,1:T(8,128)S(1)} %copy.255, f32[128]{0:T(128)} %param.15, f32[128,4,8]{0,2,1:T(8,128)S(1)} %get-tuple-element.67), kind=kLoop, calls=%fused_computation.12 | loop fusion | flops 1572864 | bytes 3162624 | tf_op jit(solution)/shard_map/convert_element_type | solution.py:48
  62.6 2.4 %fusion.52 = f32[8,128,256]{1,2,0:T(8,128)} fusion(pred[128,256]{0,1:T(8,128)(4,1)} %concatenate.30, bf16[128,4,8,128]{3,0,2,1:T(8,128)(2,1)} %multiply_convert_fusion, bf16[128,4,128]{2,0,1:T(8,128)(2,1)S(1)} %copy.253, bf16[128,4,128]{2,0,1:T(8,128)(2,1)S(1)} %copy.254), kind=kOutput, calls=%fused_computation.89 | convolution fusion | flops 68027648 | bytes 1605632 | tf_op jit(solution)/shard_map/div | solution.py:67
  65.0 2.4 %fusion.54 = f32[8,128,256]{1,2,0:T(8,128)} fusion(pred[128,256]{0,1:T(8,128)(4,1)} %concatenate.30, bf16[128,4,8,128]{3,0,2,1:T(8,128)(2,1)} %multiply_convert_fusion, bf16[128,4,128]{2,0,1:T(8,128)(2,1)S(1)} %copy.253, bf16[128,4,128]{2,0,1:T(8,128)(2,1)S(1)} %copy.254), kind=kOutput, calls=%fused_computation.91 | convolution fusion | flops 68027648 | bytes 1605632 | tf_op jit(solution)/shard_map/div | solution.py:67
  67.4 2.4 %fusion.56 = f32[8,128,256]{1,2,0:T(8,128)} fusion(pred[128,256]{0,1:T(8,128)(4,1)} %concatenate.30, bf16[128,4,8,128]{3,0,2,1:T(8,128)(2,1)} %multiply_convert_fusion, bf16[128,4,128]{2,0,1:T(8,128)(2,1)S(1)} %copy.253, bf16[128,4,128]{2,0,1:T(8,128)(2,1)S(1)} %copy.254), kind=kOutput, calls=%fused_computation.93 | convolution fusion | flops 68027648 | bytes 1605632 | tf_op jit(solution)/shard_map/div | solution.py:67
  71.0 1.7 pad_maximum_fusion.2
  72.7 1.8 copy.256
  74.5 2.3 %copy.258 = bf16[128,4096]{0,1:T(8,128)(2,1)} copy(bf16[128,4096]{1,0:T(8,128)(2,1)} %param.14) | data formatting | bytes 2097152 | tf_op args[5]
  76.8 1.3 broadcast_select_fusion
  79.0 1.0 fusion.118
  80.0 1.8 copy.362
  81.9 1.8 copy.366
  83.7 1.8 copy.364
  85.5 1.8 copy.368
  87.2 2.4 %fusion.50 = f32[8,128,256]{1,2,0:T(8,128)} fusion(bf16[256,128,1]{1,0,2:T(8,128)(2,1)} %fusion.81, pred[128,256]{0,1:T(8,128)(4,1)} %concatenate.30, bf16[128,4,8,128]{3,0,2,1:T(8,128)(2,1)} %multiply_convert_fusion), kind=kOutput, calls=%fused_computation.87 | convolution fusion | flops 67896576 | bytes 1409024 | tf_op jit(solution)/shard_map/div | solution.py:67
  89.6 1.7 convolution_bitcast_fusion.8
  91.4 1.9 fusion.37
  93.3 1.2 fusion.25
  94.5 1.0 fusion.48
  96.7 1.0 fusion.46
  102.7 1.7 copy.308
  104.4 1.6 concatenate.33
  106.0 1.1 pad_maximum_fusion.1
  108.6 1.7 copy.307
  110.3 1.6 concatenate.32
  111.9 1.8 pad_maximum_fusion.3
  113.7 4.6 %all-to-all-start = ((bf16[32,4,1024]{2,1,0:T(4,128)(2,1)}), bf16[32,4,1024]{2,1,0:T(4,128)(2,1)}, u32[]{:S(2)}, u32[]{:S(2)}) async-start(bf16[32,4,1024]{2,1,0:T(4,128)(2,1)} %pad_maximum_fusion.3), calls=%async_computation | async-start | bytes 524288 | tf_op jit(solution)/shard_map/all_to_all | solution.py:36
  118.3 1.3 rsqrt.36
  119.5 1.3 reshape.178
  120.8 2.3 %fusion.33 = f32[128,1,8,128]{3,0,2,1:T(8,128)} fusion(bf16[256,128,1]{1,0,2:T(8,128)(2,1)} %fusion.81, bf16[8,128,256]{1,2,0:T(8,128)(2,1)} %copy-done.6), kind=kOutput, calls=%fused_computation.55 | convolution fusion | flops 67239936 | bytes 1114112 | tf_op jit(solution)/shard_map/gck,kd->cgd/dot_general | solution.py:68
  123.2 2.2 %fusion.34 = f32[128,1,8,128]{3,0,2,1:T(8,128)} fusion(bf16[8,128,256]{1,2,0:T(8,128)(2,1)} %copy-done.7, bf16[128,4,128]{2,0,1:T(8,128)(2,1)S(1)} %copy.253, bf16[128,4,128]{2,0,1:T(8,128)(2,1)S(1)} %copy.254), kind=kOutput, calls=%fused_computation.57 | convolution fusion | flops 67371008 | bytes 1310720 | tf_op jit(solution)/shard_map/gck,kd->cgd/dot_general | solution.py:68
  125.3 1.1 fusion.35
  126.5 1.1 fusion.36
  127.6 1.7 copy.312
  129.3 1.1 multiply_reduce_fusion.1
  130.4 1.1 multiply_convert_fusion.1
  132.3 3.6 %multiply_reduce_fusion = (f32[128,4,8]{0,2,1:T(8,128)S(1)}, f32[128,4,8,128]{3,0,2,1:T(8,128)}) fusion(f32[128,4,8,128]{3,0,2,1:T(8,128)S(1)} %copy.255, f32[128]{0:T(128)} %param.15, f32[128,4,8]{0,2,1:T(8,128)S(1)} %get-tuple-element.67, f32[128,1,8,128]{3,0,2,1:T(8,128)} %fusion.33, f32[128,1,8,128]{3,0,2,1:T(8,128)} %fusion.34, ...), kind=kLoop, calls=%fused_computation.11 | loop fusion | flops 3665920 | bytes 6324736 | tf_op jit(solution)/shard_map/reduce_sum | solution.py:53
  135.9 1.9 copy.290
  137.9 2.2 %fusion.4 = (f32[4096]{0:T(1024)S(1)}, bf16[128,4096]{0,1:T(8,128)(2,1)}) fusion(f32[128,4,8,128]{0,3,2,1:T(8,128)S(1)} %copy.290, bf16[128,4096]{0,1:T(8,128)(2,1)S(1)} %copy.250, f32[128,4,8]{0,2,1:T(8,128)S(1)} %get-tuple-element.67, f32[128,32]{0,1:T(8,128)S(1)} %multiply_bitcast_fusion, f32[4096]{0:T(1024)S(1)} %broadcast_bitcast_fusion, ...), kind=kLoop, calls=%fused_computation.8 | loop fusion | flops 5238784 | bytes 4276224 | tf_op jit(solution)/shard_map/reduce_sum | solution.py:54
  140.1 2.3 %copy.310 = bf16[128,4096]{1,0:T(8,128)(2,1)} copy(bf16[128,4096]{0,1:T(8,128)(2,1)} %get-tuple-element.55) | data formatting | bytes 2097152
  142.5 1.1 convert_reduce_fusion
  145.2 25.2 %all-reduce.1 = (f32[128]{0:T(128)S(1)}, f32[128]{0:T(128)S(1)}) all-reduce(f32[128]{0:T(128)S(1)} %bitcast_reduce_fusion.1, f32[128]{0:T(128)S(1)} %add.62), channel_id=1, replica_groups=mesh['dp_0'=12,'dp_1'=2,'group_0'=4,'group_1'=4,'group_2'=2] {'dp_0'}, use_global_device_ids=true, to_apply=%region_17.18 | all-reduce | flops 256 | bytes 2048 | tf_op jit(solution)/shard_map/psum | solution.py:41
  170.4 3.8 %all-reduce.5 = (f32[128]{0:T(128)S(1)}, f32[128]{0:T(128)S(1)}) all-reduce(f32[128]{0:T(128)S(1)} %get-tuple-element.44, f32[128]{0:T(128)S(1)} %get-tuple-element.45), channel_id=1, replica_groups=mesh['dp_0'=12,'dp_1'=2,'group_0'=4,'group_1'=4,'group_2'=2] {'dp_1'}, use_global_device_ids=true, to_apply=%region_18.19 | all-reduce | flops 256 | bytes 2048 | tf_op jit(solution)/shard_map/psum | solution.py:41
  174.1 8.5 %all-reduce.3 = (f32[128]{0:T(128)S(1)}, f32[128]{0:T(128)S(1)}) all-reduce(f32[128]{0:T(128)S(1)} %get-tuple-element.52, f32[128]{0:T(128)S(1)} %get-tuple-element.53), channel_id=1, replica_groups=mesh['dp_0'=12,'dp_1'=2,'group_0'=4,'group_1'=4,'group_2'=2] {'group_0'}, use_global_device_ids=true, to_apply=%region_19.20 | all-reduce | flops 256 | bytes 2048 | tf_op jit(solution)/shard_map/psum | solution.py:41
  182.6 10.2 %all-reduce.2 = (f32[128]{0:T(128)S(1)}, f32[128]{0:T(128)S(1)}) all-reduce(f32[128]{0:T(128)S(1)} %get-tuple-element.48, f32[128]{0:T(128)S(1)} %get-tuple-element.49), channel_id=1, replica_groups=mesh['dp_0'=12,'dp_1'=2,'group_0'=4,'group_1'=4,'group_2'=2] {'group_1'}, use_global_device_ids=true, to_apply=%region_20.21 | all-reduce | flops 256 | bytes 2048 | tf_op jit(solution)/shard_map/psum | solution.py:41
  192.8 13.7 %all-reduce.4 = (f32[128]{0:T(128)}, f32[128]{0:T(128)}) all-reduce(f32[128]{0:T(128)S(1)} %get-tuple-element.46, f32[128]{0:T(128)S(1)} %get-tuple-element.47), channel_id=1, replica_groups=mesh['dp_0'=12,'dp_1'=2,'group_0'=4,'group_1'=4,'group_2'=2] {'group_2'}, use_global_device_ids=true, to_apply=%region_21.22 | all-reduce | flops 256 | bytes 2048 | tf_op jit(solution)/shard_map/psum | solution.py:41
  (120 shorter events, 19.0 us)
Async XLA Ops:
  0.6 55.8 %copy-start.15 = (bf16[128,4096]{1,0:T(8,128)(2,1)S(1)}, bf16[128,4096]{1,0:T(8,128)(2,1)}, u32[]{:S(2)}) copy-start(bf16[128,4096]{1,0:T(8,128)(2,1)} %param.9) | copy-start | bytes 3145732
  1.9 3.7 %copy-start.26 = (f32[512]{0:T(512)}, f32[512]{0:T(512)S(1)}, u32[]{:S(2)}) copy-start(f32[512]{0:T(512)S(1)} %broadcast_bitcast_fusion.3) | copy-start | bytes 6148
  2.6 54.5 %copy-start.21 = (f32[4,4,128]{2,1,0:T(4,128)}, f32[4,4,128]{2,1,0:T(4,128)S(1)}, u32[]{:S(2)}) copy-start(f32[4,4,128]{2,1,0:T(4,128)S(1)} %reshape.175) | copy-start | bytes 24580
  2.7 1.2 copy-start.29
  2.8 1.1 copy-start.19
  3.9 1.7 copy-start.25
  78.1 1.0 copy-start
  89.6 3.6 %copy-start.1 = (bf16[128,4096]{0,1:T(8,128)(2,1)S(1)}, bf16[128,4096]{0,1:T(8,128)(2,1)}, u32[]{:S(2)}) copy-start(bf16[128,4096]{0,1:T(8,128)(2,1)} %copy-done) | copy-start | bytes 3145732
  89.6 3.6 %copy-start.5 = (f32[8,128,256]{1,2,0:T(8,128)S(1)}, f32[8,128,256]{1,2,0:T(8,128)}, u32[]{:S(2)}) copy-start(f32[8,128,256]{1,2,0:T(8,128)} %fusion.50) | copy-start | bytes 3145732
  89.6 4.9 %copy-start.12 = (bf16[128,4,8,128]{3,0,2,1:T(8,128)(2,1)S(1)}, bf16[128,4,8,128]{3,0,2,1:T(8,128)(2,1)}, u32[]{:S(2)}) copy-start(bf16[128,4,8,128]{3,0,2,1:T(8,128)(2,1)} %multiply_convert_fusion) | copy-start | bytes 3145732
  91.4 4.1 %copy-start.4 = (f32[8,128,256]{1,2,0:T(8,128)S(1)}, f32[8,128,256]{1,2,0:T(8,128)}, u32[]{:S(2)}) copy-start(f32[8,128,256]{1,2,0:T(8,128)} %fusion.52) | copy-start | bytes 3145732
  93.3 2.5 %copy-start.14 = (bf16[256,512]{0,1:T(8,128)(2,1)S(1)}, bf16[256,512]{0,1:T(8,128)(2,1)}, u32[]{:S(2)}) copy-start(bf16[256,512]{0,1:T(8,128)(2,1)} %copy.256) | copy-start | bytes 786436
  93.3 2.5 %copy-start.18 = (bf16[128,1,8,128]{3,0,2,1:T(8,128)(2,1)S(1)}, bf16[128,1,8,128]{3,0,2,1:T(8,128)(2,1)}, u32[]{:S(2)}) copy-start(bf16[128,1,8,128]{3,0,2,1:T(8,128)(2,1)} %copy.366) | copy-start | bytes 786436
  94.5 2.2 %copy-start.6 = (bf16[8,128,256]{1,2,0:T(8,128)(2,1)}, bf16[8,128,256]{1,2,0:T(8,128)(2,1)S(1)}, u32[]{:S(2)}) copy-start(bf16[8,128,256]{1,2,0:T(8,128)(2,1)S(1)} %fusion.25) | copy-start | bytes 1572868
  95.8 1.8 copy-start.3
  96.3 1.6 copy-start.17
  96.7 2.1 %copy-start.7 = (bf16[8,128,256]{1,2,0:T(8,128)(2,1)}, bf16[8,128,256]{1,2,0:T(8,128)(2,1)S(1)}, u32[]{:S(2)}) copy-start(bf16[8,128,256]{1,2,0:T(8,128)(2,1)S(1)} %fusion.26) | copy-start | bytes 1572868
  98.0 1.8 copy-start.2
  98.5 1.6 copy-start.16
  98.8 2.1 %copy-start.8 = (bf16[8,128,256]{1,2,0:T(8,128)(2,1)}, bf16[8,128,256]{1,2,0:T(8,128)(2,1)S(1)}, u32[]{:S(2)}) copy-start(bf16[8,128,256]{1,2,0:T(8,128)(2,1)S(1)} %fusion.27) | copy-start | bytes 1572868
  100.9 1.0 copy-start.10
  107.2 0.8 copy-start.13
  113.7 28.8 %all-to-all-start = ((bf16[32,4,1024]{2,1,0:T(4,128)(2,1)}), bf16[32,4,1024]{2,1,0:T(4,128)(2,1)}, u32[]{:S(2)}, u32[]{:S(2)}) async-start(bf16[32,4,1024]{2,1,0:T(4,128)(2,1)} %pad_maximum_fusion.3), calls=%async_computation | async-start | bytes 524288 | tf_op jit(solution)/shard_map/all_to_all | solution.py:36
  120.8 4.5 %copy-start.9 = (bf16[8,128,256]{1,2,0:T(8,128)(2,1)S(1)}, bf16[8,128,256]{1,2,0:T(8,128)(2,1)}, u32[]{:S(2)}) copy-start(bf16[8,128,256]{1,2,0:T(8,128)(2,1)} %copy-done.8) | copy-start | bytes 1572868
  120.8 5.7 %copy-start.11 = (bf16[8,128,256]{1,2,0:T(8,128)(2,1)S(1)}, bf16[8,128,256]{1,2,0:T(8,128)(2,1)}, u32[]{:S(2)}) copy-start(bf16[8,128,256]{1,2,0:T(8,128)(2,1)} %copy-done.10) | copy-start | bytes 1572868
  135.9 2.0 copy-start.32
  135.9 2.0 copy-start.23
  140.1 4.1 %copy-start.22 = (f32[4,4,128]{2,1,0:T(4,128)S(1)}, f32[4,4,128]{2,1,0:T(4,128)}, u32[]{:S(2)}) copy-start(f32[4,4,128]{2,1,0:T(4,128)} %copy-done.21) | copy-start | bytes 24580
  140.1 4.1 %copy-start.30 = (f32[4,4]{1,0:T(4,128)S(1)}, f32[4,4]{1,0:T(4,128)}, u32[]{:S(2)}) copy-start(f32[4,4]{1,0:T(4,128)} %copy-done.29) | copy-start | bytes 196
  140.1 4.1 %copy-start.31 = (f32[128]{0:T(128)S(1)}, f32[128]{0:T(128)}, u32[]{:S(2)}) copy-start(f32[128]{0:T(128)} %param.16) | copy-start | bytes 1540
  140.1 4.4 %copy-start.20 = (f32[1,4,4,128]{3,2,1,0:T(4,128)S(1)}, f32[1,4,4,128]{3,2,1,0:T(4,128)}, u32[]{:S(2)}) copy-start(f32[1,4,4,128]{3,2,1,0:T(4,128)} %copy-done.19) | copy-start | bytes 24580
  140.1 4.4 %copy-start.24 = (bf16[4,512]{1,0:T(4,128)(2,1)S(1)}, bf16[4,512]{1,0:T(4,128)(2,1)}, u32[]{:S(2)}) copy-start(bf16[4,512]{1,0:T(4,128)(2,1)} %param.12) | copy-start | bytes 12292
  140.1 4.3 %copy-start.27 = (f32[512]{0:T(512)S(1)}, f32[512]{0:T(512)}, u32[]{:S(2)}) copy-start(f32[512]{0:T(512)} %copy-done.26) | copy-start | bytes 6148
  140.1 5.0 %copy-start.28 = (f32[16,128]{1,0:T(8,128)S(1)}, f32[16,128]{1,0:T(8,128)}, u32[]{:S(2)}) copy-start(f32[16,128]{1,0:T(8,128)} %reshape.178) | copy-start | bytes 24580
  140.1 4.9 %copy-start.33 = (f32[16]{0:T(128)S(1)}, f32[16]{0:T(128)}, u32[]{:S(2)}) copy-start(f32[16]{0:T(128)} %rsqrt.36) | copy-start | bytes 196
where the time goes:
time: 208 us; the launch traced here: 207 us
  blocking collectives  111 us (53%)
  local copies, waits for them, and re-layouts  38.2 us (18%)
  matrix products  28.3 us (14%)
  other arithmetic  22.3 us (11%)
  starting transfers between devices  4.56 us (2%)
    psum x5, blocking collectives, by_axis(): return functools.reduce(lax.psum, axes, x)  61.4 us
    all_gather x1, blocking collectives, side_by_side(): lax.all_gather(both, axis, axis=dim, tiled=True)  49.8 us
    unnamed x81, local copies, waits for them, and re-layouts  18 us
    div x4, matrix products, head_grads(): dscore = (expo / totals * (dprob - delta)).astype(jnp.bfloat16)  9.55 us
    dot_general x4, matrix products, head_grads(): jnp.einsum('gck,kd->cgd', dscore, key_head, preferred_element_type=jnp.fl...  6.79 us
    all_to_all x1, starting transfers between devices, sent_and_summed(): lax.all_to_all(blocks, axis, split_axis=0, concat_axis=0, tiled=True)  4.56 us
  transfers between devices with their start and end apart: 1, of which 0 were waited for; matrix products, arithmetic and copies ran while one was open for 12% of the time, Pallas kernels for 0%

commit v1 on v0

v1 whole, which is shorter than its diff:
```python
import functools

import jax
import jax.numpy as jnp
from jax import lax
from jax.experimental import pallas as pl
from jax.experimental.pallas import tpu as pltpu
from jax.sharding import Mesh
from jax.sharding import PartitionSpec as P

HD = 128
HQ = 32
HK = 4
PER = HQ // HK
TOK = 128
SHARD = 4
PEERS = 32
REPLICAS = 24
EPS = 1e-06
SCALE = HD ** (-0.5)
LOG2E = 1.4426950408889634
GROUP = ("group_0", "group_1", "group_2")
DP = ("dp_0", "dp_1")
DP_GROUP = ("dp_0", "dp_1", "group_0", "group_1", "group_2")
NT = (((1,), (1,)), ((), ()))
TN = (((0,), (0,)), ((), ()))
NN = (((1,), (0,)), ((), ()))


def dot(a, b, dims):
    return lax.dot_general(a, b, dims, preferred_element_type=jnp.float32)


def unit_of(x):
    wide = x.astype(jnp.float32)
    inverse = lax.rsqrt(jnp.mean(wide * wide, axis=-1, keepdims=True) + EPS)
    return wide * inverse, inverse


def back_of(grad, unit, inverse, gain):
    scaled = grad * gain
    return inverse * (scaled - unit * jnp.mean(scaled * unit, axis=-1, keepdims=True))


def rows_eight(x):
    return jnp.sum(x.reshape(x.shape[0] // 8, 8, x.shape[1]), axis=0)


def unmix(mixed):
    pairs = mixed.reshape(PEERS // 2, 2, 8, HD)
    even, odd = pairs[:, 0], pairs[:, 1]
    low = lax.broadcasted_iota(jnp.int32, even.shape, 1) < SHARD
    first = jnp.where(low, even, pltpu.roll(odd, SHARD, 1))
    second = jnp.where(low, pltpu.roll(even, SHARD, 1), odd)
    return first.reshape(TOK, HD), second.reshape(TOK, HD)


def mix(first, second):
    one = first.reshape(PEERS // 2, 8, HD)
    two = second.reshape(PEERS // 2, 8, HD)
    low = lax.broadcasted_iota(jnp.int32, one.shape, 1) < SHARD
    even = jnp.where(low, one, pltpu.roll(two, SHARD, 1))
    odd = jnp.where(low, pltpu.roll(one, SHARD, 1), two)
    return jnp.stack([even, odd], axis=1).reshape(PEERS, 8, HD)


def pieces(x):
    high = x.astype(jnp.bfloat16).astype(jnp.float32)
    middle = (x - high).astype(jnp.bfloat16).astype(jnp.float32)
    return [high, middle, x - high - middle]


def attention_kernel(
    len_ref, q_ref, do_ref, ck_ref, cv_ref, pkv_ref, qg_ref, kg_ref,
    dq_ref, dck_ref, dcv_ref, term_ref,
    qn_s, g_s, p_s, ds_s, acc_s,
):
    step = pl.program_id(0)
    qg = qg_ref[...]
    kg = kg_ref[...]

    @pl.when(step == 0)
    def _():
        acc_s[...] = jnp.zeros_like(acc_s)

    pk, pv = unmix(pkv_ref[...].astype(jnp.float32))
    kraw = jnp.concatenate([pk, ck_ref[...].astype(jnp.float32)], axis=0)
    kunit, kinv = unit_of(kraw)
    kn = (kunit * kg).astype(jnp.bfloat16)
    v = jnp.concatenate([pv.astype(jnp.bfloat16), cv_ref[...]], axis=0)

    live = lax.broadcasted_iota(jnp.int32, (TOK, HD), 0) < len_ref[0]
    for j in range(PER):
        cols, rows = pl.ds(j * HD, HD), pl.ds(j * TOK, TOK)
        qunit, _ = unit_of(q_ref[:, cols])
        qn_s[rows, :] = (qunit * qg).astype(jnp.bfloat16)
        g_s[rows, :] = jnp.where(live, do_ref[:, cols].astype(jnp.float32), 0.0).astype(jnp.bfloat16)

    key = lax.broadcasted_iota(jnp.int32, (TOK, 2 * TOK), 0)
    slot = lax.rem(lax.broadcasted_iota(jnp.int32, (TOK, 2 * TOK), 1), TOK)
    seen = key <= slot
    qacc = jnp.zeros((8, HD), jnp.float32)
    for pair in range(PER // 2):
        span = pl.ds(pair * 2 * TOK, 2 * TOK)
        qn, g = qn_s[span, :], g_s[span, :]
        score = dot(kn, qn, NT) * (SCALE * LOG2E)
        dprob = dot(v, g, NT)
        expo = jnp.exp2(score)
        expo = jnp.concatenate([expo[:TOK], jnp.where(seen, expo[TOK:], 0.0)], axis=0)
        total = jnp.sum(expo, axis=0, keepdims=True)
        weighted = jnp.sum(expo * dprob, axis=0, keepdims=True)
        inv = 1.0 / total
        prob = expo * inv
        dscore = (prob * (dprob - weighted * inv)).astype(jnp.bfloat16)
        p_s[:, span] = prob.astype(jnp.bfloat16)
        ds_s[:, span] = dscore
        dn = dot(dscore, kn, TN) * SCALE
        for half in range(2):
            cols = pl.ds((pair * 2 + half) * HD, HD)
            unit, inverse = unit_of(q_ref[:, cols])
            grad = dn[half * TOK : (half + 1) * TOK]
            dq_ref[:, cols] = back_of(grad, unit, inverse, qg).astype(jnp.bfloat16)
            qacc += rows_eight(grad * unit)

    dv = dot(p_s[...], g_s[...], NN)
    dk = dot(ds_s[...], qn_s[...], NN) * SCALE
    dck_ref[...] = back_of(dk[TOK:], kunit[TOK:], kinv[TOK:], kg).astype(jnp.bfloat16)
    dcv_ref[...] = dv[TOK:].astype(jnp.bfloat16)
    here = pl.ds(pl.multiple_of(step * HD, HD), HD)
    term_ref[:, :, here] = mix(dk[:TOK], dv[:TOK]).astype(jnp.bfloat16)
    acc_s[0:8, :] += qacc
    acc_s[8:16, :] += rows_eight(dk * kunit)

    @pl.when(step == HK - 1)
    def _():
        rows = pieces(jnp.sum(acc_s[0:8, :], axis=0, keepdims=True))
        rows += pieces(jnp.sum(acc_s[8:16, :], axis=0, keepdims=True))
        rows += [jnp.zeros((2, HD), jnp.float32)]
        tile = jnp.broadcast_to(jnp.concatenate(rows, axis=0)[None], (PEERS, 8, HD))
        term_ref[:, :, HK * HD :] = tile.astype(jnp.bfloat16)


def attention(lengths, query, d_out, comp_key, comp_value, prompt, q_gain, k_gain):
    wide = pl.BlockSpec((TOK, PER * HD), lambda h, *_: (0, h))
    narrow = pl.BlockSpec((TOK, HD), lambda h, *_: (0, h))
    mixed = pl.BlockSpec((PEERS, 8, HD), lambda h, *_: (0, 0, h))
    gain = pl.BlockSpec((1, HD), lambda h, *_: (0, 0))
    whole = pl.BlockSpec((PEERS, 8, (HK + 1) * HD), lambda h, *_: (0, 0, 0))
    return pl.pallas_call(
        attention_kernel,
        grid_spec=pltpu.PrefetchScalarGridSpec(
            num_scalar_prefetch=1,
            grid=(HK,),
            in_specs=[wide, wide, narrow, narrow, mixed, gain, gain],
            out_specs=[wide, narrow, narrow, whole],
            scratch_shapes=[
                pltpu.VMEM((PER * TOK, HD), jnp.bfloat16),
                pltpu.VMEM((PER * TOK, HD), jnp.bfloat16),
                pltpu.VMEM((2 * TOK, PER * TOK), jnp.bfloat16),
                pltpu.VMEM((2 * TOK, PER * TOK), jnp.bfloat16),
                pltpu.VMEM((16, HD), jnp.float32),
            ],
        ),
        out_shape=[
            jax.ShapeDtypeStruct((TOK, HQ * HD), jnp.bfloat16),
            jax.ShapeDtypeStruct((TOK, HK * HD), jnp.bfloat16),
            jax.ShapeDtypeStruct((TOK, HK * HD), jnp.bfloat16),
            jax.ShapeDtypeStruct((PEERS, 8, (HK + 1) * HD), jnp.bfloat16),
        ],
        cost_estimate=pl.CostEstimate(
            flops=5 * 2 * HQ * TOK * 2 * TOK * HD, bytes_accessed=5 << 20, transcendentals=HQ * TOK * 2 * TOK
        ),
        compiler_params=pltpu.CompilerParams(dimension_semantics=("arbitrary",)),
        name="attention_back",
    )(lengths, query, d_out, comp_key, comp_value, prompt, q_gain.reshape(1, HD), k_gain.reshape(1, HD))


def pack_kernel(key_ref, value_ref, out_ref):
    own = jnp.concatenate([key_ref[...].astype(jnp.float32), value_ref[...].astype(jnp.float32)], axis=0)
    out_ref[...] = jnp.broadcast_to(own.astype(jnp.bfloat16)[None], out_ref.shape)


def pack(prompt_key, prompt_value):
    return pl.pallas_call(
        pack_kernel,
        out_shape=jax.ShapeDtypeStruct((PEERS, 8, HK * HD), jnp.bfloat16),
        name="prompt_pack",
    )(prompt_key, prompt_value)


def finish_kernel(arrived_ref, key_ref, kg_ref, dk_ref, dv_ref, gain_ref):
    both = jnp.sum(arrived_ref[...].astype(jnp.float32), axis=0)
    tail = both[:, HK * HD :]
    for row in range(2):
        total = tail[3 * row : 3 * row + 1] + (tail[3 * row + 1 : 3 * row + 2] + tail[3 * row + 2 : 3 * row + 3])
        gain_ref[:, row : row + 1, :] = jnp.broadcast_to(total[None], (REPLICAS, 1, HD))
    for h in range(HK):
        cols = pl.ds(h * HD, HD)
        unit, inverse = unit_of(key_ref[:, cols])
        grad = both[:SHARD, h * HD : (h + 1) * HD]
        dk_ref[:, cols] = back_of(grad, unit, inverse, kg_ref[...]).astype(jnp.bfloat16)
    dv_ref[...] = both[SHARD:, : HK * HD].astype(jnp.bfloat16)


def finish(arrived, prompt_key, k_gain):
    out = jax.ShapeDtypeStruct((SHARD, HK * HD), jnp.bfloat16)
    gains = jax.ShapeDtypeStruct((REPLICAS, 2, HD), jnp.float32)
    return pl.pallas_call(finish_kernel, out_shape=[out, out, gains], name="prompt_back")(
        arrived, prompt_key, k_gain.reshape(1, HD)
    )


def exchange(x, axes):
    return lax.all_to_all(x, axes, split_axis=0, concat_axis=0, tiled=True)


def local(query, comp_key, comp_value, prompt_key, prompt_value, d_out, q_gain, k_gain, lengths):
    prompt = exchange(pack(prompt_key, prompt_value), GROUP)
    dq, dck, dcv, term = attention(
        lengths, query, d_out, comp_key, comp_value, prompt, q_gain, k_gain
    )
    dpk, dpv, gains = finish(exchange(term, GROUP), prompt_key, k_gain)
    gains = jnp.sum(exchange(gains, DP), axis=0)
    return (dq, dck, dcv, dpk, dpv, gains[0], gains[1])


def solution(mesh):
    finer = Mesh(
        mesh.devices.reshape(12, 2, 4, 4, 2), ("dp_0", "dp_1", "group_0", "group_1", "group_2")
    )
    rows = P(DP_GROUP, None)
    return jax.shard_map(
        local,
        mesh=finer,
        in_specs=(rows, rows, rows, rows, rows, rows, P(), P(), P(DP_GROUP)),
        out_specs=(rows, rows, rows, rows, rows, P(), P()),
        check_vma=False,
    )
```

time: 208 us -> 84.3 us (0.41)
  blocking collectives: 111 us -> 41.1 us
  local copies, waits for them, and re-layouts: 38.2 us -> 1.22 us
  matrix products: 28.3 us -> 0 us
  other arithmetic: 22.3 us -> 0.04 us
  Pallas kernels: 0 us -> 14.2 us
  waiting for transfers between devices: 0.01 us -> 12 us
  starting transfers between devices: 4.56 us -> 14 us
    psum x5 -> x0, blocking collectives: 61.4 us -> none  [by_axis(): return functools.reduce(lax.psum, axes, x)]
    all_gather x1 -> x0, blocking collectives: 49.8 us -> none  [side_by_side(): lax.all_gather(both, axis, axis=dim, tiled=True)]
    all_to_all x0 -> x2, blocking collectives: none -> 41.1 us  [exchange(): return lax.all_to_all(x, axes, split_axis=0, concat_axis=0, tiled=True)]
    dot_general x20 -> x0, matrix products: 18.8 us -> none  [the longest x4 6.79 us: head_grads(): jnp.einsum('gck,kd->cgd', dscore, key_head, preferred_element_type=jnp.fl...]
    unnamed x81 -> x2, local copies, waits for them, and re-layouts: 18 us -> 0.7 us
    pallas_call x0 -> x3, Pallas kernels: none -> 14.2 us  [the longest x1 11.1 us: attention(): pl.pallas_call(attention_kernel, grid_spec=pltpu.PrefetchScalarGridSpec(n...]
    all_to_all x1, waiting for transfers between devices: 0.01 us -> 12 us  [exchange(): return lax.all_to_all(x, axes, split_axis=0, concat_axis=0, tiled=True)]
    div x4 -> x0, matrix products: 9.55 us -> none  [head_grads(): dscore = (expo / totals * (dprob - delta)).astype(jnp.bfloat16)]
  transfers between devices with their start and end apart: 1 -> 1, of which waited for: 0 -> 1; matrix products, arithmetic and copies ran while one was open for 12% -> 0% of each run, Pallas kernels for 0% -> 0%
where the time goes in v1:
time: 84.3 us; the launch traced here: 83.9 us
  blocking collectives  41.1 us (49%)
  Pallas kernels  14.2 us (17%)
  starting transfers between devices  14 us (17%)
  waiting for transfers between devices  12 us (14%)
  between operations  1.3 us (2%)
  local copies, waits for them, and re-layouts  1.22 us (1%)
    all_to_all x2, blocking collectives, exchange(): return lax.all_to_all(x, axes, split_axis=0, concat_axis=0, tiled=True)  41.1 us
    all_to_all x1, starting transfers between devices, exchange(): return lax.all_to_all(x, axes, split_axis=0, concat_axis=0, tiled=True)  14 us
    all_to_all x1, waiting for transfers between devices, exchange(): return lax.all_to_all(x, axes, split_axis=0, concat_axis=0, tiled=True)  12 us
    pallas_call x1, Pallas kernels, attention(): pl.pallas_call(attention_kernel, grid_spec=pltpu.PrefetchScalarGridSpec(n...  11.1 us
    pallas_call x1, Pallas kernels, finish(): pl.pallas_call(finish_kernel, out_shape=[out, out, gains], name='prompt_b...  1.76 us
  transfers between devices with their start and end apart: 1, of which 1 were waited for; matrix products, arithmetic and copies ran while one was open for 0% of the time, Pallas kernels for 0%

profile of v1, /device:TPU:1, one launch (start us, length us, event | category | flops | bytes accessed | tf_op | source)
XLA Modules:
  0.0 83.9 jit_solution(1535927203612490817)
XLA Ops:
  0.6 1.4 %prompt_pack.1 = bf16[32,8,512]{2,1,0:T(8,128)(2,1)} custom-call(bf16[4,512]{1,0:T(4,128)(2,1)} %key_ref.3, bf16[4,512]{1,0:T(4,128)(2,1)} %value_ref.1), custom_call_target="tpu_custom_call" | custom-call | tf_op jit(solution)/shard_map/prompt_pack/pallas_call | solution.py:184
  2.1 14.0 %all-to-all-start = ((bf16[32,8,512]{2,1,0:T(8,128)(2,1)}), bf16[32,8,512]{2,1,0:T(8,128)(2,1)S(1)}, u32[]{:S(2)}, u32[]{:S(2)}) async-start(bf16[32,8,512]{2,1,0:T(8,128)(2,1)} %prompt_pack.1), calls=%async_computation | async-start | bytes 524288 | tf_op jit(solution)/shard_map/all_to_all | solution.py:214
  16.7 12.0 %all-to-all-done.pkv_ref = bf16[32,8,512]{2,1,0:T(8,128)(2,1)S(1)} async-done(((bf16[32,8,512]{2,1,0:T(8,128)(2,1)}), bf16[32,8,512]{2,1,0:T(8,128)(2,1)S(1)}, u32[]{:S(2)}, u32[]{:S(2)}) %all-to-all-start) | async-done | bytes 262176 | tf_op jit(solution)/shard_map/all_to_all | solution.py:214
  28.7 0.0 copy-start
  28.7 0.7 copy-done
  29.4 11.1 %attention_back.1 = (bf16[128,4096]{1,0:T(8,128)(2,1)}, bf16[128,512]{1,0:T(8,128)(2,1)}, bf16[128,512]{1,0:T(8,128)(2,1)}, bf16[32,8,640]{2,1,0:T(8,128)(2,1)}) custom-call(s32[1]{0:T(128)S(6)} %copy.16.len_ref, bf16[128,4096]{1,0:T(8,128)(2,1)} %q_ref.1, bf16[128,4096]{1,0:T(8,128)(2,1)} %do_ref.1, bf16[128,512]{1,0:T(8,128)(2,1)} %ck_ref.1, ...), custom_call_target="tpu_custom_call" | custom-call | flops 1342177280 | bytes 5242880 | tf_op jit(solution)/shard_map/attention_back/pallas_call | solution.py:149
  40.5 18.3 %all_to_all.15.arrived_ref = bf16[32,8,640]{2,1,0:T(8,128)(2,1)} all-to-all(bf16[32,8,640]{2,1,0:T(8,128)(2,1)} %get-tuple-element.17), channel_id=1, replica_groups=mesh['dp_0'=12,'dp_1'=2,'group_0'=4,'group_1'=4,'group_2'=2] {'group_0',..., dimensions={0} | all-to-all | bytes 655360 | tf_op jit(solution)/shard_map/all_to_all | solution.py:214
  58.8 1.8 %prompt_back.1 = (bf16[4,512]{1,0:T(4,128)(2,1)}, bf16[4,512]{1,0:T(4,128)(2,1)}, f32[24,2,128]{2,1,0:T(2,128)}) custom-call(bf16[32,8,640]{2,1,0:T(8,128)(2,1)} %all_to_all.15.arrived_ref, bf16[4,512]{1,0:T(4,128)(2,1)} %key_ref.3, f32[1,128]{1,0:T(1,128)} %bitcast.7), custom_call_target="tpu_custom_call" | custom-call | tf_op jit(solution)/shard_map/prompt_back/pallas_call | solution.py:208
  60.6 22.7 %all_to_all.16 = f32[24,2,128]{2,1,0:T(2,128)S(1)} all-to-all(f32[24,2,128]{2,1,0:T(2,128)} %get-tuple-element.20), channel_id=1, replica_groups=mesh['dp_0'=12,'dp_1'=2,'group_0'=4,'group_1'=4,'group_2'=2] {'dp_0','dp..., dimensions={0} | all-to-all | bytes 49152 | tf_op jit(solution)/shard_map/all_to_all | solution.py:214
  83.4 0.5 slice_bitcast_fusion
  (1 shorter events, 0.0 us)
Async XLA Ops:
  2.1 26.7 %all-to-all-start = ((bf16[32,8,512]{2,1,0:T(8,128)(2,1)}), bf16[32,8,512]{2,1,0:T(8,128)(2,1)S(1)}, u32[]{:S(2)}, u32[]{:S(2)}) async-start(bf16[32,8,512]{2,1,0:T(8,128)(2,1)} %prompt_pack.1), calls=%async_computation | async-start | bytes 524288 | tf_op jit(solution)/shard_map/all_to_all | solution.py:214
  28.7 0.7 copy-start

commit v2 on v1

v2 whole, which is shorter than its diff:
```python
import functools

import jax
import jax.numpy as jnp
from jax import lax
from jax.experimental import pallas as pl
from jax.experimental.pallas import tpu as pltpu
from jax.sharding import Mesh
from jax.sharding import PartitionSpec as P

HD = 128
HQ = 32
HK = 4
PER = HQ // HK
TOK = 128
SHARD = 4
PEERS = 32
PLACES = PEERS // 2
REPLICAS = 48
EPS = 1e-06
SCALE = HD ** (-0.5)
LOG2E = 1.4426950408889634
GROUP = ("group_0", "group_1", "group_2")
CORE = "group_2"
PLACE = ("group_0", "group_1")
DP_CORE = ("dp_0", "dp_1", "group_2")
DP_GROUP = ("dp_0", "dp_1", "group_0", "group_1", "group_2")
NT = (((1,), (1,)), ((), ()))
TN = (((0,), (0,)), ((), ()))
NN = (((1,), (0,)), ((), ()))


def dot(a, b, dims):
    return lax.dot_general(a, b, dims, preferred_element_type=jnp.float32)


def unit_of(x):
    wide = x.astype(jnp.float32)
    inverse = lax.rsqrt(jnp.mean(wide * wide, axis=-1, keepdims=True) + EPS)
    return wide * inverse, inverse


def back_of(grad, unit, inverse, gain):
    scaled = grad * gain
    return inverse * (scaled - unit * jnp.mean(scaled * unit, axis=-1, keepdims=True))


def rows_eight(x):
    return jnp.sum(x.reshape(x.shape[0] // 8, 8, x.shape[1]), axis=0)


def unmix(mixed):
    pairs = mixed.reshape(PEERS // 2, 2, 8, HD)
    even, odd = pairs[:, 0], pairs[:, 1]
    low = lax.broadcasted_iota(jnp.int32, even.shape, 1) < SHARD
    first = jnp.where(low, even, pltpu.roll(odd, SHARD, 1))
    second = jnp.where(low, pltpu.roll(even, SHARD, 1), odd)
    return first.reshape(TOK, HD), second.reshape(TOK, HD)


def mix(first, second):
    one = first.reshape(PEERS // 2, 8, HD)
    two = second.reshape(PEERS // 2, 8, HD)
    low = lax.broadcasted_iota(jnp.int32, one.shape, 1) < SHARD
    even = jnp.where(low, one, pltpu.roll(two, SHARD, 1))
    odd = jnp.where(low, pltpu.roll(one, SHARD, 1), two)
    return even, odd


def pieces(x):
    high = x.astype(jnp.bfloat16).astype(jnp.float32)
    middle = (x - high).astype(jnp.bfloat16).astype(jnp.float32)
    return [high, middle, x - high - middle]


def params(mib, *semantics):
    return pltpu.CompilerParams(vmem_limit_bytes=int(mib * 2**20), dimension_semantics=semantics or None)


def pack_kernel(key_ref, value_ref, out_ref):
    own = jnp.concatenate([key_ref[...].astype(jnp.float32), value_ref[...].astype(jnp.float32)], axis=0)
    out_ref[...] = jnp.broadcast_to(own.astype(jnp.bfloat16)[None], out_ref.shape)


def pack(prompt_key, prompt_value):
    return pl.pallas_call(
        pack_kernel,
        out_shape=jax.ShapeDtypeStruct((PEERS, 8, HK * HD), jnp.bfloat16),
        compiler_params=params(4),
        name="prompt_pack",
    )(prompt_key, prompt_value)


def own_kernel(len_ref, q_ref, do_ref, ck_ref, cv_ref, qg_ref, kg_ref, qn_ref, g_ref, e_ref, dp_ref, sums_ref):
    live = lax.broadcasted_iota(jnp.int32, (TOK, HD), 0) < len_ref[0]
    kunit, _ = unit_of(ck_ref[...])
    kn = (kunit * kg_ref[...]).astype(jnp.bfloat16)
    v = cv_ref[...]
    key = lax.broadcasted_iota(jnp.int32, (TOK, 2 * TOK), 0)
    slot = lax.rem(lax.broadcasted_iota(jnp.int32, (TOK, 2 * TOK), 1), TOK)
    seen = key <= slot
    for pair in range(PER // 2):
        span = pl.ds(pair * 2 * TOK, 2 * TOK)
        for j in (2 * pair, 2 * pair + 1):
            cols, rows = pl.ds(j * HD, HD), pl.ds(j * TOK, TOK)
            qunit, _ = unit_of(q_ref[:, cols])
            qn_ref[rows, :] = (qunit * qg_ref[...]).astype(jnp.bfloat16)
            g_ref[rows, :] = jnp.where(live, do_ref[:, cols].astype(jnp.float32), 0.0).astype(jnp.bfloat16)
        expo = jnp.exp2(dot(kn, qn_ref[span, :], NT) * (SCALE * LOG2E))
        expo = jnp.where(seen, expo, 0.0)
        dprob = dot(v, g_ref[span, :], NT)
        e_ref[0, :, span] = expo.astype(jnp.bfloat16)
        dp_ref[0, :, span] = dprob.astype(jnp.bfloat16)
        sums_ref[0, 0:1, span] = jnp.sum(expo, axis=0, keepdims=True)
        sums_ref[0, 1:2, span] = jnp.sum(expo * dprob, axis=0, keepdims=True)


QUERIES = PER * TOK
WIDE = pl.BlockSpec((TOK, PER * HD), lambda h, *_: (0, h))
NARROW = pl.BlockSpec((TOK, HD), lambda h, *_: (0, h))
MIXED = pl.BlockSpec((PEERS, 8, HD), lambda h, *_: (0, 0, h))
GAIN = pl.BlockSpec((1, HD), lambda h, *_: (0, 0))
STACK = pl.BlockSpec((QUERIES, HD), lambda h, *_: (h, 0))


def per_head(rows, columns):
    return pl.BlockSpec((1, rows, columns), lambda h, *_: (h, 0, 0))


def own(lengths, query, d_out, comp_key, comp_value, q_gain, k_gain):
    return pl.pallas_call(
        own_kernel,
        grid_spec=pltpu.PrefetchScalarGridSpec(
            num_scalar_prefetch=1,
            grid=(HK,),
            in_specs=[WIDE, WIDE, NARROW, NARROW, GAIN, GAIN],
            out_specs=[STACK, STACK, per_head(TOK, QUERIES), per_head(TOK, QUERIES), per_head(2, QUERIES)],
        ),
        out_shape=[
            jax.ShapeDtypeStruct((HQ * TOK, HD), jnp.bfloat16),
            jax.ShapeDtypeStruct((HQ * TOK, HD), jnp.bfloat16),
            jax.ShapeDtypeStruct((HK, TOK, QUERIES), jnp.bfloat16),
            jax.ShapeDtypeStruct((HK, TOK, QUERIES), jnp.bfloat16),
            jax.ShapeDtypeStruct((HK, 2, QUERIES), jnp.float32),
        ],
        cost_estimate=pl.CostEstimate(
            flops=2 * 2 * HQ * TOK * TOK * HD, bytes_accessed=8 << 20, transcendentals=HQ * TOK * TOK
        ),
        compiler_params=params(24, "arbitrary"),
        name="own_scores",
    )(lengths, query, d_out, comp_key, comp_value, q_gain, k_gain)


def all_keys(pk, ck, kg_ref):
    raw = jnp.concatenate([pk, ck.astype(jnp.float32)], axis=0)
    unit, inverse = unit_of(raw)
    return unit, inverse, (unit * kg_ref[...]).astype(jnp.bfloat16)


def score_kernel(
    core_ref, qn_hbm, g_hbm, e_hbm, d_hbm, sums_hbm, ck_hbm, pkv_hbm, qg_ref, kg_ref,
    ds_hbm, dck_ref, dcv_ref, keep_ref, send_ref, gain_ref,
    sums_ref, ck_ref, pkv_ref, qn_s, g_s, e_s, d_s, p_s, ds_s, acc_s, all_sem, in_sem, out_sem,
):
    pairs = ((pkv_hbm, pkv_ref), (ck_hbm, ck_ref), (sums_hbm, sums_ref))
    common = [pltpu.make_async_copy(s, t, all_sem.at[n]) for n, (s, t) in enumerate(pairs)]
    for copy in common:
        copy.start()
    def loads(h):
        rows = pl.ds(pl.multiple_of(h * QUERIES, QUERIES), QUERIES)
        sources = (qn_hbm.at[rows], g_hbm.at[rows], e_hbm.at[h], d_hbm.at[h])
        targets = (qn_s.at[h], g_s.at[h], e_s.at[h], d_s.at[h])
        return [pltpu.make_async_copy(s, t, in_sem.at[h, n]) for n, (s, t) in enumerate(zip(sources, targets))]

    def store(h):
        return pltpu.make_async_copy(ds_s.at[h], ds_hbm.at[h], out_sem.at[h])

    for h in range(HK):
        for copy in loads(h):
            copy.start()
    first_core = core_ref[0] == 0
    acc_s[...] = jnp.zeros_like(acc_s)
    for copy in common:
        copy.wait()

    def head(h, carry):
        cols = pl.ds(pl.multiple_of(h * HD, HD), HD)
        pk, pv = unmix(pkv_ref[:, :, cols].astype(jnp.float32))
        unit, inverse, kn = all_keys(pk, ck_ref[:, cols], kg_ref)
        v = pv.astype(jnp.bfloat16)
        for copy in loads(h):
            copy.wait()
        for pair in range(PER // 2):
            span = pl.ds(pair * 2 * TOK, 2 * TOK)
            expo = jnp.exp2(dot(kn[:TOK], qn_s[h, span, :], NT) * (SCALE * LOG2E))
            dprob = dot(v, g_s[h, span, :], NT)
            inv = 1.0 / (sums_ref[h, 0:1, span] + jnp.sum(expo, axis=0, keepdims=True))
            delta = (sums_ref[h, 1:2, span] + jnp.sum(expo * dprob, axis=0, keepdims=True)) * inv
            for half in range(2):
                rows = pl.ds(half * TOK, TOK)
                e = e_s[h, :, span].astype(jnp.float32) if half else expo
                d = d_s[h, :, span].astype(jnp.float32) if half else dprob
                prob = e * inv
                p_s[rows, span] = prob.astype(jnp.bfloat16)
                ds_s[h, rows, span] = (prob * (d - delta)).astype(jnp.bfloat16)
        ds_s[h, :, QUERIES:] = kn
        store(h).start()
        dk = dot(ds_s[h, :, :QUERIES], qn_s[h], NN) * SCALE
        dv = dot(p_s[...], g_s[h], NN)
        acc_s[0:8, :] += rows_eight(dk * kn.astype(jnp.float32))
        acc_s[8:16, :] += rows_eight(dk * unit)
        dck_ref[:, cols] = back_of(dk[TOK:], unit[TOK:], inverse[TOK:], kg_ref[...]).astype(jnp.bfloat16)
        dcv_ref[:, cols] = dv[TOK:].astype(jnp.bfloat16)
        zero, one = mix(dk[:TOK], dv[:TOK])
        keep_ref[:, :, cols] = jnp.where(first_core, zero, one).astype(jnp.bfloat16)
        send_ref[:, :, cols] = jnp.where(first_core, one, zero).astype(jnp.bfloat16)
        return carry

    for h in range(HK):
        head(h, 0)
    rows = [jnp.sum(acc_s[0:8, :], axis=0, keepdims=True) / qg_ref[...]]
    rows += [jnp.sum(acc_s[8:16, :], axis=0, keepdims=True)]
    gain_ref[...] = jnp.broadcast_to(jnp.concatenate(rows, axis=0)[None], gain_ref.shape)
    for h in range(HK):
        store(h).wait()


VMEM = pl.BlockSpec(memory_space=pltpu.VMEM)
ANY = pl.BlockSpec(memory_space=pl.ANY)


def scores(core, qn, g, e, dp, sums, comp_key, prompt, q_gain, k_gain):
    half = jax.ShapeDtypeStruct((PLACES, 8, HK * HD), jnp.bfloat16)
    return pl.pallas_call(
        score_kernel,
        in_specs=[pl.BlockSpec(memory_space=pltpu.SMEM)] + [ANY] * 7 + [VMEM] * 2,
        out_specs=[ANY] + [VMEM] * 5,
        out_shape=[
            jax.ShapeDtypeStruct((HK, 2 * TOK, QUERIES + HD), jnp.bfloat16),
            jax.ShapeDtypeStruct((TOK, HK * HD), jnp.bfloat16),
            jax.ShapeDtypeStruct((TOK, HK * HD), jnp.bfloat16),
            half,
            half,
            jax.ShapeDtypeStruct((REPLICAS, 2, HD), jnp.float32),
        ],
        scratch_shapes=[
            pltpu.VMEM((HK, 2, QUERIES), jnp.float32),
            pltpu.VMEM((TOK, HK * HD), jnp.bfloat16),
            pltpu.VMEM((PEERS, 8, HK * HD), jnp.bfloat16),
            pltpu.VMEM((HK, QUERIES, HD), jnp.bfloat16),
            pltpu.VMEM((HK, QUERIES, HD), jnp.bfloat16),
            pltpu.VMEM((HK, TOK, QUERIES), jnp.bfloat16),
            pltpu.VMEM((HK, TOK, QUERIES), jnp.bfloat16),
            pltpu.VMEM((2 * TOK, QUERIES), jnp.bfloat16),
            pltpu.VMEM((HK, 2 * TOK, QUERIES + HD), jnp.bfloat16),
            pltpu.VMEM((16, HD), jnp.float32),
            pltpu.SemaphoreType.DMA((3,)),
            pltpu.SemaphoreType.DMA((HK, 4)),
            pltpu.SemaphoreType.DMA((HK,)),
        ],
        cost_estimate=pl.CostEstimate(
            flops=6 * 2 * HQ * TOK * TOK * HD, bytes_accessed=7 << 20, transcendentals=HQ * TOK * TOK
        ),
        compiler_params=params(50.75),
        name="all_scores",
    )(core, qn, g, e, dp, sums, comp_key, prompt, q_gain, k_gain)


def query_kernel(ds_ref, q_ref, qg_ref, dq_ref):
    kn = ds_ref[0, :, QUERIES:]
    for pair in range(PER // 2):
        dn = dot(ds_ref[0, :, pair * 2 * TOK : (pair + 1) * 2 * TOK], kn, TN) * SCALE
        for half in range(2):
            cols = pl.ds((pair * 2 + half) * HD, HD)
            unit, inverse = unit_of(q_ref[:, cols])
            grad = dn[half * TOK : (half + 1) * TOK]
            dq_ref[:, cols] = back_of(grad, unit, inverse, qg_ref[...]).astype(jnp.bfloat16)


def queries_back(ds, query, q_gain):
    return pl.pallas_call(
        query_kernel,
        grid=(HK,),
        in_specs=[per_head(2 * TOK, QUERIES + HD), WIDE, GAIN],
        out_specs=WIDE,
        out_shape=jax.ShapeDtypeStruct((TOK, HQ * HD), jnp.bfloat16),
        cost_estimate=pl.CostEstimate(
            flops=2 * 2 * HQ * TOK * TOK * HD, bytes_accessed=5 << 20, transcendentals=0
        ),
        compiler_params=params(60, "arbitrary"),
        name="query_back",
    )(ds, query, q_gain)


def join_kernel(keep_ref, got_ref, out_ref):
    total = keep_ref[...].astype(jnp.float32) + got_ref[...].astype(jnp.float32)
    out_ref[:, :, : HK * HD] = total.astype(jnp.bfloat16)


def join(keep, got):
    return pl.pallas_call(
        join_kernel,
        out_shape=jax.ShapeDtypeStruct((PLACES, 8, (HK + 1) * HD), jnp.bfloat16),
        cost_estimate=pl.CostEstimate(flops=1 << 17, bytes_accessed=400 << 10, transcendentals=0),
        compiler_params=params(4),
        name="core_join",
    )(keep, got)


def relay_kernel(arrived_ref, joined_hbm, out_ref):
    both = jnp.sum(arrived_ref[...], axis=0)
    rows = pieces(both[0:1]) + pieces(both[1:2]) + [jnp.zeros((2, HD), jnp.float32)]
    tile = jnp.concatenate(rows, axis=0)[None]
    out_ref[...] = jnp.broadcast_to(tile, out_ref.shape).astype(jnp.bfloat16)


def relay(arrived, joined):
    return pl.pallas_call(
        relay_kernel,
        grid=(1,),
        in_specs=[pl.BlockSpec((REPLICAS, 2, HD), lambda i: (0, 0, 0)), ANY],
        out_specs=pl.BlockSpec((PLACES, 8, HD), lambda i: (0, 0, HK)),
        out_shape=jax.ShapeDtypeStruct(joined.shape, joined.dtype),
        input_output_aliases={1: 0},
        compiler_params=params(4),
        name="gain_relay",
    )(arrived, joined)


def finish_kernel(arrived_ref, key_ref, kg_ref, dk_ref, dv_ref, gq_ref, gk_ref):
    both = jnp.sum(arrived_ref[...].astype(jnp.float32), axis=0)
    for row, ref in ((0, gq_ref), (3, gk_ref)):
        high, middle, low = [both[row + n : row + n + 1, HK * HD :] for n in range(3)]
        ref[...] = high + (middle + low)
    for h in range(HK):
        cols = pl.ds(h * HD, HD)
        unit, inverse = unit_of(key_ref[:, cols])
        grad = both[:SHARD, h * HD : (h + 1) * HD]
        dk_ref[:, cols] = back_of(grad, unit, inverse, kg_ref[...]).astype(jnp.bfloat16)
    dv_ref[...] = both[SHARD:, : HK * HD].astype(jnp.bfloat16)


def finish(arrived, prompt_key, k_gain):
    out = jax.ShapeDtypeStruct((SHARD, HK * HD), jnp.bfloat16)
    gain = jax.ShapeDtypeStruct((1, HD), jnp.float32)
    return pl.pallas_call(
        finish_kernel,
        out_shape=[out, out, gain, gain],
        cost_estimate=pl.CostEstimate(flops=1 << 20, bytes_accessed=300 << 10, transcendentals=0),
        compiler_params=params(4),
        name="prompt_back",
    )(arrived, prompt_key, k_gain)


def exchange(x, axes):
    return lax.all_to_all(x, axes, split_axis=0, concat_axis=0, tiled=True)


def local(query, comp_key, comp_value, prompt_key, prompt_value, d_out, q_gain, k_gain, lengths):
    q_gain, k_gain = q_gain.reshape(1, HD), k_gain.reshape(1, HD)
    core = lax.axis_index(CORE).reshape(1)
    prompt = exchange(pack(prompt_key, prompt_value), GROUP)
    owned = own(lengths, query, d_out, comp_key, comp_value, q_gain, k_gain)
    ds, dck, dcv, keep, send, gains = scores(core, *owned, comp_key, prompt, q_gain, k_gain)
    gains = exchange(gains, DP_CORE)
    joined = join(keep, lax.ppermute(send, CORE, [(0, 1), (1, 0)]))
    dq = queries_back(ds, query, q_gain)
    dpk, dpv, gain_q, gain_k = finish(exchange(relay(gains, joined), PLACE), prompt_key, k_gain)
    return (dq, dck, dcv, dpk, dpv, gain_q.reshape(HD), gain_k.reshape(HD))


def solution(mesh):
    finer = Mesh(
        mesh.devices.reshape(12, 2, 4, 4, 2), ("dp_0", "dp_1", "group_0", "group_1", "group_2")
    )
    rows = P(DP_GROUP, None)
    return jax.shard_map(
        local,
        mesh=finer,
        in_specs=(rows, rows, rows, rows, rows, rows, P(), P(), P(DP_GROUP)),
        out_specs=(rows, rows, rows, rows, rows, P(), P()),
        check_vma=False,
    )
```

time: 84.3 us -> 79.3 us (0.941)
  blocking collectives: 41.1 us -> 0 us
  starting transfers between devices: 14 us -> 36.5 us
  local copies, waits for them, and re-layouts: 1.22 us -> 8.93 us
  Pallas kernels: 14.2 us -> 17.4 us
  waiting for transfers between devices: 12 us -> 14.5 us
    all_to_all x2 -> x0, blocking collectives: 41.1 us -> none  [exchange(): return lax.all_to_all(x, axes, split_axis=0, concat_axis=0, tiled=True)]
    all_to_all x1 -> x3, starting transfers between devices: 14 us -> 34.2 us  [exchange(): return lax.all_to_all(x, axes, split_axis=0, concat_axis=0, tiled=True)]
    unnamed x2 -> x28, local copies, waits for them, and re-layouts: 0.7 us -> 8.93 us
    pallas_call x2 -> x6, Pallas kernels: 12.8 us -> 16.7 us  [the longest x1 6.23 us: scores(): pl.pallas_call(score_kernel, in_specs=[pl.BlockSpec(memory_space=pltpu.SM...]
    ppermute x0 -> x1, starting transfers between devices: none -> 2.25 us  [local(): joined = join(keep, lax.ppermute(send, CORE, [(0, 1), (1, 0)]))]
    all_to_all x1 -> x3, waiting for transfers between devices: 12 us -> 13.5 us  [exchange(): return lax.all_to_all(x, axes, split_axis=0, concat_axis=0, tiled=True)]
    ppermute x0 -> x1, waiting for transfers between devices: none -> 0.98 us  [local(): joined = join(keep, lax.ppermute(send, CORE, [(0, 1), (1, 0)]))]
  transfers between devices with their start and end apart: 1 -> 4, of which waited for: 1 -> 4; matrix products, arithmetic and copies ran while one was open for 0% -> 0% of each run, Pallas kernels for 0% -> 11%
where the time goes in v2:
time: 79.3 us; the launch traced here: 78.7 us
  starting transfers between devices  36.5 us (46%)
  Pallas kernels  17.4 us (22%)
  waiting for transfers between devices  14.5 us (18%)
  local copies, waits for them, and re-layouts  8.93 us (11%)
  between operations  1.38 us (2%)
    all_to_all x3, starting transfers between devices, exchange(): return lax.all_to_all(x, axes, split_axis=0, concat_axis=0, tiled=True)  34.2 us
    all_to_all x3, waiting for transfers between devices, exchange(): return lax.all_to_all(x, axes, split_axis=0, concat_axis=0, tiled=True)  13.5 us
    unnamed x28, local copies, waits for them, and re-layouts  8.93 us
    pallas_call x1, Pallas kernels, scores(): pl.pallas_call(score_kernel, in_specs=[pl.BlockSpec(memory_space=pltpu.SM...  6.23 us
    pallas_call x1, Pallas kernels, queries_back(): pl.pallas_call(query_kernel, grid=(HK,), in_specs=[per_head(2 * TOK, QUER...  6.04 us
    pallas_call x1, Pallas kernels, own(): pl.pallas_call(own_kernel, grid_spec=pltpu.PrefetchScalarGridSpec(num_sca...  2.27 us
    ppermute x1, starting transfers between devices, local(): joined = join(keep, lax.ppermute(send, CORE, [(0, 1), (1, 0)]))  2.25 us
  transfers between devices with their start and end apart: 4, of which 4 were waited for; matrix products, arithmetic and copies ran while one was open for 0% of the time, Pallas kernels for 11%

profile of v2, /device:TPU:1, one launch (start us, length us, event | category | flops | bytes accessed | tf_op | source)
XLA Modules:
  0.0 78.7 jit_solution(12402675039026248573)
XLA Ops:
  0.6 0.0 copy-start.5
  0.6 0.0 copy-start.7
  0.7 0.7 copy-done.7
  1.4 0.0 copy-start.13
  1.4 0.7 copy-done.13
  2.1 0.0 copy-start.10
  2.1 0.0 copy-start.12
  2.1 0.7 prompt_pack.1
  2.8 14.0 %all-to-all-start = ((bf16[32,8,512]{2,1,0:T(8,128)(2,1)}), bf16[32,8,512]{2,1,0:T(8,128)(2,1)S(1)}, u32[]{:S(2)}, u32[]{:S(2)}) async-start(bf16[32,8,512]{2,1,0:T(8,128)(2,1)} %prompt_pack.1), calls=%async_computation | async-start | bytes 524288 | tf_op jit(solution)/shard_map/all_to_all | solution.py:356
  17.4 0.0 copy-start
  17.4 1.2 %copy-done = bf16[128,4096]{1,0:T(8,128)(2,1)S(1)} copy-done((bf16[128,4096]{1,0:T(8,128)(2,1)S(1)}, bf16[128,4096]{1,0:T(8,128)(2,1)}, u32[]{:S(2)}) %copy-start) | copy-done | bytes 1048600
  18.7 0.0 copy-start.1
  18.7 1.2 %copy-done.1 = bf16[128,4096]{1,0:T(8,128)(2,1)S(1)} copy-done((bf16[128,4096]{1,0:T(8,128)(2,1)S(1)}, bf16[128,4096]{1,0:T(8,128)(2,1)}, u32[]{:S(2)}) %copy-start.1) | copy-done | bytes 1048600
  19.9 0.0 copy-start.4
  19.9 0.9 %copy-done.4 = bf16[128,512]{1,0:T(8,128)(2,1)S(1)} copy-done((bf16[128,512]{1,0:T(8,128)(2,1)S(1)}, bf16[128,512]{1,0:T(8,128)(2,1)}, u32[]{:S(2)}) %copy-start.4) | copy-done | bytes 131096
  20.8 0.0 copy-start.6
  20.8 0.9 %copy-done.6 = bf16[128,512]{1,0:T(8,128)(2,1)S(1)} copy-done((bf16[128,512]{1,0:T(8,128)(2,1)S(1)}, bf16[128,512]{1,0:T(8,128)(2,1)}, u32[]{:S(2)}) %copy-start.6) | copy-done | bytes 131096
  21.7 0.0 copy-start.9
  21.7 0.7 copy-done.9
  22.4 0.0 copy-start.11
  22.4 0.7 copy-done.11
  23.0 2.3 %own_scores.1 = (bf16[4096,128]{1,0:T(8,128)(2,1)S(1)}, bf16[4096,128]{1,0:T(8,128)(2,1)S(1)}, bf16[4,128,1024]{2,1,0:T(8,128)(2,1)S(1)}, bf16[4,128,1024]{2,1,0:T(8,128)(2,1)S(1)}, f32[4,2,1024]{2,1,0:T(2,128)S(1)}) custom-call(s32[1]{0:T(128)S(6)} %copy.18.len_ref, bf16[128,4096]{1,0:T(8,128)(2,1)S(1)} %copy-done, bf16[128,4096]{1,0:T(8,128)(2,1)S(1)} %copy-done.1, ...), custom_call_target="tpu_custom_call" | custom-call | flops 268435456 | bytes 8388608 | tf_op jit(solution)/shard_map/own_scores/pallas_call | solution.py:131
  25.3 0.0 copy-start.2
  25.3 1.0 %copy-done.2 = bf16[4,128,1024]{2,1,0:T(8,128)(2,1)} copy-done((bf16[4,128,1024]{2,1,0:T(8,128)(2,1)}, bf16[4,128,1024]{2,1,0:T(8,128)(2,1)S(1)}, u32[]{:S(2)}) %copy-start.2) | copy-done | bytes 1048600
  26.3 0.0 copy-start.3
  26.3 1.0 %copy-done.3 = bf16[4,128,1024]{2,1,0:T(8,128)(2,1)} copy-done((bf16[4,128,1024]{2,1,0:T(8,128)(2,1)}, bf16[4,128,1024]{2,1,0:T(8,128)(2,1)S(1)}, u32[]{:S(2)}) %copy-start.3) | copy-done | bytes 1048600
  27.2 2.2 %all-to-all-done.pkv_hbm = bf16[32,8,512]{2,1,0:T(8,128)(2,1)S(1)} async-done(((bf16[32,8,512]{2,1,0:T(8,128)(2,1)}), bf16[32,8,512]{2,1,0:T(8,128)(2,1)S(1)}, u32[]{:S(2)}, u32[]{:S(2)}) %all-to-all-start) | async-done | bytes 262176 | tf_op jit(solution)/shard_map/all_to_all | solution.py:356
  29.4 0.0 copy-done.5
  29.4 0.0 copy-done.10
  29.4 0.0 copy-done.12
  29.4 6.2 %all_scores.1 = (bf16[4,256,1152]{2,1,0:T(8,128)(2,1)}, bf16[128,512]{1,0:T(8,128)(2,1)}, bf16[128,512]{1,0:T(8,128)(2,1)}, bf16[16,8,512]{2,1,0:T(8,128)(2,1)S(...) custom-call(s32[1]{0:T(128)} %bitcast.core_ref, bf16[4096,128]{1,0:T(8,128)(2,1)S(1)} %get-tuple-element.22.qn_hbm, ...), custom_call_target="tpu_custom_call" | custom-call | flops 805306368 | bytes 7340032 | tf_op jit(solution)/shard_map/all_scores/pallas_call | solution.py:234
  35.7 13.5 %all-to-all-start.1 = ((f32[48,2,128]{2,1,0:T(2,128)}), f32[48,2,128]{2,1,0:T(2,128)S(1)}, u32[]{:S(2)}, u32[]{:S(2)}) async-start(f32[48,2,128]{2,1,0:T(2,128)} %get-tuple-element.30), calls=%async_computation.1 | async-start | bytes 98304 | tf_op jit(solution)/shard_map/all_to_all | solution.py:356
  49.2 2.3 %collective-permute-start = (bf16[16,8,512]{2,1,0:T(8,128)(2,1)S(1)}, bf16[16,8,512]{2,1,0:T(8,128)(2,1)S(1)}, u32[]{:S(2)}, u32[]{:S(2)}) collective-permute-start(bf16[16,8,512]{2,1,0:T(8,128)(2,1)S(1)} %get-tuple-element.32), channel_id=1, source_target_pairs={{0,1},{1,0},{2,3},{3,2},{4,5},{5,4},{6,7},{7,6},{8,9},{9,8},{10,11... | collective-permute-start | bytes 393224 | tf_op jit(solution)/shard_map/ppermute | solution.py:366
  51.4 1.0 %collective-permute-done.got_ref = bf16[16,8,512]{2,1,0:T(8,128)(2,1)S(1)} collective-permute-done((bf16[16,8,512]{2,1,0:T(8,128)(2,1)S(1)}, bf16[16,8,512]{2,1,0:T(8,128)(2,1)S(1)}, u32[]{:S(2)}, u32[]{:S(2)}) %collective-permute-start) | collective-permute-done | bytes 131104 | tf_op jit(solution)/shard_map/ppermute | solution.py:366
  52.4 0.7 core_join.1.joined_hbm
  53.1 6.8 %all-to-all-done.1.arrived_ref = f32[48,2,128]{2,1,0:T(2,128)S(1)} async-done(((f32[48,2,128]{2,1,0:T(2,128)}), f32[48,2,128]{2,1,0:T(2,128)S(1)}, u32[]{:S(2)}, u32[]{:S(2)}) %all-to-all-start.1) | async-done | bytes 49184 | tf_op jit(solution)/shard_map/all_to_all | solution.py:356
  59.9 0.7 gain_relay.1
  60.6 0.0 copy-start.8
  60.6 6.7 %all-to-all-start.2 = ((bf16[16,8,640]{2,1,0:T(8,128)(2,1)}), bf16[16,8,640]{2,1,0:T(8,128)(2,1)S(1)}, u32[]{:S(2)}, u32[]{:S(2)}) async-start(bf16[16,8,640]{2,1,0:T(8,128)(2,1)} %gain_relay.1), calls=%async_computation.2 | async-start | bytes 327680 | tf_op jit(solution)/shard_map/all_to_all | solution.py:356
  67.4 6.0 %query_back.1 = bf16[128,4096]{1,0:T(8,128)(2,1)} custom-call(bf16[4,256,1152]{2,1,0:T(8,128)(2,1)} %get-tuple-element.27.ds_ref, bf16[128,4096]{1,0:T(8,128)(2,1)} %q_ref.3, f32[1,128]{1,0:T(1,128)} %bitcast.5), custom_call_target="tpu_custom_call" | custom-call | flops 268435456 | bytes 5242880 | tf_op jit(solution)/shard_map/query_back/pallas_call | solution.py:281
  73.4 4.5 %all-to-all-done.2.arrived_ref = bf16[16,8,640]{2,1,0:T(8,128)(2,1)S(1)} async-done(((bf16[16,8,640]{2,1,0:T(8,128)(2,1)}), bf16[16,8,640]{2,1,0:T(8,128)(2,1)S(1)}, u32[]{:S(2)}, u32[]{:S(2)}) %all-to-all-start.2) | async-done | bytes 163872 | tf_op jit(solution)/shard_map/all_to_all | solution.py:356
  77.9 0.0 copy-done.8
  77.9 0.8 prompt_back.1
Async XLA Ops:
  0.6 28.8 %copy-start.5 = (bf16[128,512]{1,0:T(8,128)(2,1)S(1)}, bf16[128,512]{1,0:T(8,128)(2,1)}, u32[]{:S(2)}) copy-start(bf16[128,512]{1,0:T(8,128)(2,1)} %ck_hbm.1) | copy-start | bytes 393220
  0.6 0.7 copy-start.7
  1.4 0.7 copy-start.13
  2.1 27.4 %copy-start.10 = (f32[128]{0:T(128)S(1)}, f32[128]{0:T(128)}, u32[]{:S(2)}) copy-start(f32[128]{0:T(128)} %param.15) | copy-start | bytes 1540
  2.1 27.4 %copy-start.12 = (f32[128]{0:T(128)S(1)}, f32[128]{0:T(128)}, u32[]{:S(2)}) copy-start(f32[128]{0:T(128)} %param.16) | copy-start | bytes 1540
  2.8 26.7 %all-to-all-start = ((bf16[32,8,512]{2,1,0:T(8,128)(2,1)}), bf16[32,8,512]{2,1,0:T(8,128)(2,1)S(1)}, u32[]{:S(2)}, u32[]{:S(2)}) async-start(bf16[32,8,512]{2,1,0:T(8,128)(2,1)} %prompt_pack.1), calls=%async_computation | async-start | bytes 524288 | tf_op jit(solution)/shard_map/all_to_all | solution.py:356
  17.4 1.2 %copy-start = (bf16[128,4096]{1,0:T(8,128)(2,1)S(1)}, bf16[128,4096]{1,0:T(8,128)(2,1)}, u32[]{:S(2)}) copy-start(bf16[128,4096]{1,0:T(8,128)(2,1)} %q_ref.3) | copy-start | bytes 3145732
  18.7 1.2 %copy-start.1 = (bf16[128,4096]{1,0:T(8,128)(2,1)S(1)}, bf16[128,4096]{1,0:T(8,128)(2,1)}, u32[]{:S(2)}) copy-start(bf16[128,4096]{1,0:T(8,128)(2,1)} %do_ref.1) | copy-start | bytes 3145732
  19.9 0.9 %copy-start.4 = (bf16[128,512]{1,0:T(8,128)(2,1)S(1)}, bf16[128,512]{1,0:T(8,128)(2,1)}, u32[]{:S(2)}) copy-start(bf16[128,512]{1,0:T(8,128)(2,1)} %ck_hbm.1) | copy-start | bytes 393220
  20.8 0.9 %copy-start.6 = (bf16[128,512]{1,0:T(8,128)(2,1)S(1)}, bf16[128,512]{1,0:T(8,128)(2,1)}, u32[]{:S(2)}) copy-start(bf16[128,512]{1,0:T(8,128)(2,1)} %cv_ref.1) | copy-start | bytes 393220
  21.7 0.7 copy-start.9
  22.4 0.7 copy-start.11
  25.3 1.0 %copy-start.2 = (bf16[4,128,1024]{2,1,0:T(8,128)(2,1)}, bf16[4,128,1024]{2,1,0:T(8,128)(2,1)S(1)}, u32[]{:S(2)}) copy-start(bf16[4,128,1024]{2,1,0:T(8,128)(2,1)S(1)} %get-tuple-element.24.e_hbm) | copy-start | bytes 3145732
  26.3 1.0 %copy-start.3 = (bf16[4,128,1024]{2,1,0:T(8,128)(2,1)}, bf16[4,128,1024]{2,1,0:T(8,128)(2,1)S(1)}, u32[]{:S(2)}) copy-start(bf16[4,128,1024]{2,1,0:T(8,128)(2,1)S(1)} %get-tuple-element.25.d_hbm) | copy-start | bytes 3145732
  35.7 24.2 %all-to-all-start.1 = ((f32[48,2,128]{2,1,0:T(2,128)}), f32[48,2,128]{2,1,0:T(2,128)S(1)}, u32[]{:S(2)}, u32[]{:S(2)}) async-start(f32[48,2,128]{2,1,0:T(2,128)} %get-tuple-element.30), calls=%async_computation.1 | async-start | bytes 98304 | tf_op jit(solution)/shard_map/all_to_all | solution.py:356
  49.2 3.2 %collective-permute-start = (bf16[16,8,512]{2,1,0:T(8,128)(2,1)S(1)}, bf16[16,8,512]{2,1,0:T(8,128)(2,1)S(1)}, u32[]{:S(2)}, u32[]{:S(2)}) collective-permute-start(bf16[16,8,512]{2,1,0:T(8,128)(2,1)S(1)} %get-tuple-element.32), channel_id=1, source_target_pairs={{0,1},{1,0},{2,3},{3,2},{4,5},{5,4},{6,7},{7,6},{8,9},{9,8},{10,11... | collective-permute-start | bytes 393224 | tf_op jit(solution)/shard_map/ppermute | solution.py:366
  60.6 17.3 %copy-start.8 = (bf16[4,512]{1,0:T(4,128)(2,1)S(1)}, bf16[4,512]{1,0:T(4,128)(2,1)}, u32[]{:S(2)}) copy-start(bf16[4,512]{1,0:T(4,128)(2,1)} %key_ref.3) | copy-start | bytes 12292
  60.6 17.3 %all-to-all-start.2 = ((bf16[16,8,640]{2,1,0:T(8,128)(2,1)}), bf16[16,8,640]{2,1,0:T(8,128)(2,1)S(1)}, u32[]{:S(2)}, u32[]{:S(2)}) async-start(bf16[16,8,640]{2,1,0:T(8,128)(2,1)} %gain_relay.1), calls=%async_computation.2 | async-start | bytes 327680 | tf_op jit(solution)/shard_map/all_to_all | solution.py:356

commit v3 on v2

v3 whole, which is shorter than its diff:
```python
import functools

import jax
import jax.numpy as jnp
from jax import lax
from jax.experimental import pallas as pl
from jax.experimental.pallas import tpu as pltpu
from jax.sharding import Mesh
from jax.sharding import PartitionSpec as P

HD = 128
HQ = 32
HK = 4
PER = HQ // HK
TOK = 128
SHARD = 4
PEERS = 32
PLACES = PEERS // 2
REPLICAS = 48
SCORE_MIB = 51
EPS = 1e-06
SCALE = HD ** (-0.5)
LOG2E = 1.4426950408889634
GROUP = ("group_0", "group_1", "group_2")
CORE = "group_2"
PLACE = ("group_0", "group_1")
DP_CORE = ("dp_0", "dp_1", "group_2")
DP_GROUP = ("dp_0", "dp_1", "group_0", "group_1", "group_2")
NT = (((1,), (1,)), ((), ()))
TN = (((0,), (0,)), ((), ()))
NN = (((1,), (0,)), ((), ()))


def dot(a, b, dims):
    return lax.dot_general(a, b, dims, preferred_element_type=jnp.float32)


def unit_of(x):
    wide = x.astype(jnp.float32)
    inverse = lax.rsqrt(jnp.mean(wide * wide, axis=-1, keepdims=True) + EPS)
    return wide * inverse, inverse


def back_of(grad, unit, inverse, gain):
    scaled = grad * gain
    return inverse * (scaled - unit * jnp.mean(scaled * unit, axis=-1, keepdims=True))


def rows_eight(x):
    return jnp.sum(x.reshape(x.shape[0] // 8, 8, x.shape[1]), axis=0)


def unmix(mixed):
    pairs = mixed.reshape(PEERS // 2, 2, 8, HD)
    even, odd = pairs[:, 0], pairs[:, 1]
    low = lax.broadcasted_iota(jnp.int32, even.shape, 1) < SHARD
    first = jnp.where(low, even, pltpu.roll(odd, SHARD, 1))
    second = jnp.where(low, pltpu.roll(even, SHARD, 1), odd)
    return first.reshape(TOK, HD), second.reshape(TOK, HD)


def mix(first, second):
    one = first.reshape(PEERS // 2, 8, HD)
    two = second.reshape(PEERS // 2, 8, HD)
    low = lax.broadcasted_iota(jnp.int32, one.shape, 1) < SHARD
    even = jnp.where(low, one, pltpu.roll(two, SHARD, 1))
    odd = jnp.where(low, pltpu.roll(one, SHARD, 1), two)
    return even, odd


def pieces(x):
    high = x.astype(jnp.bfloat16).astype(jnp.float32)
    middle = (x - high).astype(jnp.bfloat16).astype(jnp.float32)
    return [high, middle, x - high - middle]


def params(mib, *semantics):
    return pltpu.CompilerParams(vmem_limit_bytes=int(mib * 2**20), dimension_semantics=semantics or None)


def pack_kernel(key_ref, value_ref, out_ref):
    own = jnp.concatenate([key_ref[...].astype(jnp.float32), value_ref[...].astype(jnp.float32)], axis=0)
    out_ref[...] = jnp.broadcast_to(own.astype(jnp.bfloat16)[None], out_ref.shape)


def pack(prompt_key, prompt_value):
    return pl.pallas_call(
        pack_kernel,
        out_shape=jax.ShapeDtypeStruct((PEERS, 8, HK * HD), jnp.bfloat16),
        compiler_params=params(60),
        name="prompt_pack",
    )(prompt_key, prompt_value)


def own_kernel(len_ref, q_ref, do_ref, qg_ref, qn_ref, g_ref):
    live = lax.broadcasted_iota(jnp.int32, (TOK, HD), 0) < len_ref[0]
    for j in range(PER):
        cols, rows = pl.ds(j * HD, HD), pl.ds(j * TOK, TOK)
        qunit, _ = unit_of(q_ref[:, cols])
        qn_ref[rows, :] = (qunit * qg_ref[...]).astype(jnp.bfloat16)
        g_ref[rows, :] = jnp.where(live, do_ref[:, cols].astype(jnp.float32), 0.0).astype(jnp.bfloat16)


QUERIES = PER * TOK
WIDE = pl.BlockSpec((TOK, PER * HD), lambda h, *_: (0, h))
NARROW = pl.BlockSpec((TOK, HD), lambda h, *_: (0, h))
MIXED = pl.BlockSpec((PEERS, 8, HD), lambda h, *_: (0, 0, h))
GAIN = pl.BlockSpec((1, HD), lambda h, *_: (0, 0))
STACK = pl.BlockSpec((QUERIES, HD), lambda h, *_: (h, 0))


def per_head(rows, columns):
    return pl.BlockSpec((1, rows, columns), lambda h, *_: (h, 0, 0))


def own(lengths, query, d_out, q_gain):
    stacked = jax.ShapeDtypeStruct((HQ * TOK, HD), jnp.bfloat16)
    return pl.pallas_call(
        own_kernel,
        grid_spec=pltpu.PrefetchScalarGridSpec(
            num_scalar_prefetch=1,
            grid=(HK,),
            in_specs=[WIDE, WIDE, GAIN],
            out_specs=[STACK, STACK],
        ),
        out_shape=[stacked, stacked],
        cost_estimate=pl.CostEstimate(flops=1 << 24, bytes_accessed=4 << 20, transcendentals=HQ * TOK),
        compiler_params=params(24, "arbitrary"),
        name="own_norms",
    )(lengths, query, d_out, q_gain)


def all_keys(pk, ck, kg_ref):
    raw = jnp.concatenate([pk, ck.astype(jnp.float32)], axis=0)
    unit, inverse = unit_of(raw)
    return unit, inverse, (unit * kg_ref[...]).astype(jnp.bfloat16)


def score_kernel(
    core_ref, qn_ref, g_ref, ck_ref, cv_ref, pkv_ref, qg_ref, kg_ref,
    ds_hbm, dck_ref, dcv_ref, keep_ref, send_ref, gain_ref,
    p_s, ds_s, out_sem,
):
    stores = [pltpu.make_async_copy(ds_s.at[h], ds_hbm.at[h], out_sem.at[h]) for h in range(HK)]
    first_core = core_ref[0] == 0
    key = lax.broadcasted_iota(jnp.int32, (TOK, 2 * TOK), 0)
    slot = lax.rem(lax.broadcasted_iota(jnp.int32, (TOK, 2 * TOK), 1), TOK)
    seen = key <= slot
    qgain = jnp.zeros((8, HD), jnp.float32)
    kgain = jnp.zeros((8, HD), jnp.float32)
    for h in range(HK):
        cols = pl.ds(h * HD, HD)
        pk, pv = unmix(pkv_ref[:, :, cols].astype(jnp.float32))
        unit, inverse, kn = all_keys(pk, ck_ref[:, cols], kg_ref)
        v = jnp.concatenate([pv.astype(jnp.bfloat16), cv_ref[:, cols]], axis=0)
        for pair in range(PER // 2):
            span = pl.ds(pair * 2 * TOK, 2 * TOK)
            rows = pl.ds((h * PER + pair * 2) * TOK, 2 * TOK)
            expo = jnp.exp2(dot(kn, qn_ref[rows, :], NT) * (SCALE * LOG2E))
            expo = jnp.concatenate([expo[:TOK], jnp.where(seen, expo[TOK:], 0.0)], axis=0)
            dprob = dot(v, g_ref[rows, :], NT)
            inv = 1.0 / jnp.sum(expo, axis=0, keepdims=True)
            delta = jnp.sum(expo * dprob, axis=0, keepdims=True) * inv
            prob = expo * inv
            p_s[h, :, span] = prob.astype(jnp.bfloat16)
            ds_s[h, :, span] = (prob * (dprob - delta)).astype(jnp.bfloat16)
        ds_s[h, :, QUERIES:] = kn
        stores[h].start()
        rows = pl.ds(h * QUERIES, QUERIES)
        dv = dot(p_s[h], g_ref[rows, :], NN)
        dk = dot(ds_s[h, :, :QUERIES], qn_ref[rows, :], NN) * SCALE
        qgain += rows_eight(dk * kn.astype(jnp.float32))
        kgain += rows_eight(dk * unit)
        dck_ref[:, cols] = back_of(dk[TOK:], unit[TOK:], inverse[TOK:], kg_ref[...]).astype(jnp.bfloat16)
        dcv_ref[:, cols] = dv[TOK:].astype(jnp.bfloat16)
        zero, one = mix(dk[:TOK], dv[:TOK])
        keep_ref[:, :, cols] = jnp.where(first_core, zero, one).astype(jnp.bfloat16)
        send_ref[:, :, cols] = jnp.where(first_core, one, zero).astype(jnp.bfloat16)
    rows = [jnp.sum(qgain, axis=0, keepdims=True) / qg_ref[...], jnp.sum(kgain, axis=0, keepdims=True)]
    gain_ref[...] = jnp.broadcast_to(jnp.concatenate(rows, axis=0)[None], gain_ref.shape)
    for copy in stores:
        copy.wait()


VMEM = pl.BlockSpec(memory_space=pltpu.VMEM)
ANY = pl.BlockSpec(memory_space=pl.ANY)


def scores(core, qn, g, comp_key, comp_value, prompt, q_gain, k_gain):
    half = jax.ShapeDtypeStruct((PLACES, 8, HK * HD), jnp.bfloat16)
    narrow = jax.ShapeDtypeStruct((TOK, HK * HD), jnp.bfloat16)
    return pl.pallas_call(
        score_kernel,
        in_specs=[pl.BlockSpec(memory_space=pltpu.SMEM)] + [VMEM] * 7,
        out_specs=[ANY] + [VMEM] * 5,
        out_shape=[
            jax.ShapeDtypeStruct((HK, 2 * TOK, QUERIES + HD), jnp.bfloat16),
            narrow,
            narrow,
            half,
            half,
            jax.ShapeDtypeStruct((REPLICAS, 2, HD), jnp.float32),
        ],
        scratch_shapes=[
            pltpu.VMEM((HK, 2 * TOK, QUERIES), jnp.bfloat16),
            pltpu.VMEM((HK, 2 * TOK, QUERIES + HD), jnp.bfloat16),
            pltpu.SemaphoreType.DMA((HK,)),
        ],
        cost_estimate=pl.CostEstimate(
            flops=8 * 2 * HQ * TOK * TOK * HD, bytes_accessed=5 << 20, transcendentals=2 * HQ * TOK * TOK
        ),
        compiler_params=params(SCORE_MIB),
        name="all_scores",
    )(core, qn, g, comp_key, comp_value, prompt, q_gain, k_gain)


def query_kernel(ds_ref, q_ref, qg_ref, dq_ref):
    kn = ds_ref[0, :, QUERIES:]
    for pair in range(PER // 2):
        dn = dot(ds_ref[0, :, pair * 2 * TOK : (pair + 1) * 2 * TOK], kn, TN) * SCALE
        for half in range(2):
            cols = pl.ds((pair * 2 + half) * HD, HD)
            unit, inverse = unit_of(q_ref[:, cols])
            grad = dn[half * TOK : (half + 1) * TOK]
            dq_ref[:, cols] = back_of(grad, unit, inverse, qg_ref[...]).astype(jnp.bfloat16)


def queries_back(part, ds, query, q_gain, filled):
    heads = HK // 2
    wide = pl.BlockSpec((TOK, PER * HD), lambda h: (0, h + part * heads))
    more = [] if filled is None else [filled]
    return pl.pallas_call(
        query_kernel if filled is None else lambda a, b, c, _, d: query_kernel(a, b, c, d),
        grid=(heads,),
        in_specs=[
            pl.BlockSpec((1, 2 * TOK, QUERIES + HD), lambda h: (h + part * heads, 0, 0)), wide, GAIN,
        ] + [ANY] * len(more),
        out_specs=wide,
        out_shape=jax.ShapeDtypeStruct((TOK, HQ * HD), jnp.bfloat16),
        input_output_aliases={} if filled is None else {3: 0},
        cost_estimate=pl.CostEstimate(
            flops=2 * HQ * TOK * TOK * HD, bytes_accessed=5 << 19, transcendentals=0
        ),
        compiler_params=params(60, "arbitrary"),
        name="query_back",
    )(ds, query, q_gain, *more)


def join_kernel(keep_ref, got_ref, out_ref):
    total = keep_ref[...].astype(jnp.float32) + got_ref[...].astype(jnp.float32)
    out_ref[:, :, : HK * HD] = total.astype(jnp.bfloat16)


def join(keep, got):
    return pl.pallas_call(
        join_kernel,
        out_shape=jax.ShapeDtypeStruct((PLACES, 8, (HK + 1) * HD), jnp.bfloat16),
        cost_estimate=pl.CostEstimate(flops=1 << 17, bytes_accessed=400 << 10, transcendentals=0),
        compiler_params=params(4),
        name="core_join",
    )(keep, got)


def relay_kernel(arrived_ref, joined_hbm, out_ref):
    both = jnp.sum(arrived_ref[...], axis=0)
    rows = pieces(both[0:1]) + pieces(both[1:2]) + [jnp.zeros((2, HD), jnp.float32)]
    tile = jnp.concatenate(rows, axis=0)[None]
    out_ref[...] = jnp.broadcast_to(tile, out_ref.shape).astype(jnp.bfloat16)


def relay(arrived, joined):
    return pl.pallas_call(
        relay_kernel,
        grid=(1,),
        in_specs=[pl.BlockSpec((REPLICAS, 2, HD), lambda i: (0, 0, 0)), ANY],
        out_specs=pl.BlockSpec((PLACES, 8, HD), lambda i: (0, 0, HK)),
        out_shape=jax.ShapeDtypeStruct(joined.shape, joined.dtype),
        input_output_aliases={1: 0},
        compiler_params=params(4),
        name="gain_relay",
    )(arrived, joined)


def finish_kernel(arrived_ref, key_ref, kg_ref, dk_ref, dv_ref, gq_ref, gk_ref):
    both = jnp.sum(arrived_ref[...].astype(jnp.float32), axis=0)
    for row, ref in ((0, gq_ref), (3, gk_ref)):
        high, middle, low = [both[row + n : row + n + 1, HK * HD :] for n in range(3)]
        ref[...] = high + (middle + low)
    for h in range(HK):
        cols = pl.ds(h * HD, HD)
        unit, inverse = unit_of(key_ref[:, cols])
        grad = both[:SHARD, h * HD : (h + 1) * HD]
        dk_ref[:, cols] = back_of(grad, unit, inverse, kg_ref[...]).astype(jnp.bfloat16)
    dv_ref[...] = both[SHARD:, : HK * HD].astype(jnp.bfloat16)


def finish(arrived, prompt_key, k_gain):
    out = jax.ShapeDtypeStruct((SHARD, HK * HD), jnp.bfloat16)
    gain = jax.ShapeDtypeStruct((1, HD), jnp.float32)
    return pl.pallas_call(
        finish_kernel,
        out_shape=[out, out, gain, gain],
        cost_estimate=pl.CostEstimate(flops=1 << 20, bytes_accessed=300 << 10, transcendentals=0),
        compiler_params=params(4),
        name="prompt_back",
    )(arrived, prompt_key, k_gain)


def exchange(x, axes):
    return lax.all_to_all(x, axes, split_axis=0, concat_axis=0, tiled=True)


def local(query, comp_key, comp_value, prompt_key, prompt_value, d_out, q_gain, k_gain, lengths):
    q_gain, k_gain = q_gain.reshape(1, HD), k_gain.reshape(1, HD)
    core = lax.axis_index(CORE).reshape(1)
    prompt = exchange(pack(prompt_key, prompt_value), GROUP)
    qn, g = own(lengths, query, d_out, q_gain)
    ds, dck, dcv, keep, send, gains = scores(core, qn, g, comp_key, comp_value, prompt, q_gain, k_gain)
    gains = exchange(gains, DP_CORE)
    joined = join(keep, lax.ppermute(send, CORE, [(0, 1), (1, 0)]))
    dq = queries_back(0, ds, query, q_gain, None)
    gains, dq = lax.optimization_barrier((gains, dq))
    dq = queries_back(1, ds, query, q_gain, dq)
    dpk, dpv, gain_q, gain_k = finish(exchange(relay(gains, joined), PLACE), prompt_key, k_gain)
    return (dq, dck, dcv, dpk, dpv, gain_q.reshape(HD), gain_k.reshape(HD))


def solution(mesh):
    finer = Mesh(
        mesh.devices.reshape(12, 2, 4, 4, 2), ("dp_0", "dp_1", "group_0", "group_1", "group_2")
    )
    rows = P(DP_GROUP, None)
    return jax.shard_map(
        local,
        mesh=finer,
        in_specs=(rows, rows, rows, rows, rows, rows, P(), P(), P(DP_GROUP)),
        out_specs=(rows, rows, rows, rows, rows, P(), P()),
        check_vma=False,
    )
```

time: 79.3 us -> 73.8 us (0.931)
  local copies, waits for them, and re-layouts: 8.93 us -> 3.12 us
  waiting for transfers between devices: 14.5 us -> 18.4 us
  starting transfers between devices: 36.5 us -> 33.3 us
    unnamed x28 -> x16, local copies, waits for them, and re-layouts: 8.93 us -> 3.12 us
    all_to_all x3, waiting for transfers between devices: 13.5 us -> 18.4 us  [exchange(): return lax.all_to_all(x, axes, split_axis=0, concat_axis=0, tiled=True)]
    all_to_all x3, starting transfers between devices: 34.2 us -> 31.1 us  [exchange(): return lax.all_to_all(x, axes, split_axis=0, concat_axis=0, tiled=True)]
    pallas_call x1, Pallas kernels: 6.23 us -> 4.58 us  [scores(): pl.pallas_call(score_kernel, in_specs=[pl.BlockSpec(memory_space=pltpu.SM...]
    pallas_call x1 -> x2, Pallas kernels: 6.04 us -> 7.58 us  [queries_back(): pl.pallas_call(query_kernel if filled is None else lambda a, b, c, _, d:...]
    pallas_call x1, Pallas kernels: 2.27 us -> 1.27 us  [own(): pl.pallas_call(own_kernel, grid_spec=pltpu.PrefetchScalarGridSpec(num_sca...]
    ppermute x1, waiting for transfers between devices: 0.98 us -> 0.01 us  [local(): joined = join(keep, lax.ppermute(send, CORE, [(0, 1), (1, 0)]))]
  transfers between devices with their start and end apart: 4 -> 4, of which waited for: 4 -> 3; matrix products, arithmetic and copies ran while one was open for 0% -> 0% of each run, Pallas kernels for 11% -> 13%
where the time goes in v3:
time: 73.8 us; the launch traced here: 73.3 us
  starting transfers between devices  33.3 us (45%)
  waiting for transfers between devices  18.4 us (25%)
  Pallas kernels  17 us (23%)
  local copies, waits for them, and re-layouts  3.12 us (4%)
  between operations  1.4 us (2%)
    all_to_all x3, starting transfers between devices, exchange(): return lax.all_to_all(x, axes, split_axis=0, concat_axis=0, tiled=True)  31.1 us
    all_to_all x3, waiting for transfers between devices, exchange(): return lax.all_to_all(x, axes, split_axis=0, concat_axis=0, tiled=True)  18.4 us
    pallas_call x2, Pallas kernels, queries_back(): pl.pallas_call(query_kernel if filled is None else lambda a, b, c, _, d:...  7.58 us
    pallas_call x1, Pallas kernels, scores(): pl.pallas_call(score_kernel, in_specs=[pl.BlockSpec(memory_space=pltpu.SM...  4.58 us
    unnamed x16, local copies, waits for them, and re-layouts  3.12 us
    ppermute x1, starting transfers between devices, local(): joined = join(keep, lax.ppermute(send, CORE, [(0, 1), (1, 0)]))  2.25 us
  transfers between devices with their start and end apart: 4, of which 3 were waited for; matrix products, arithmetic and copies ran while one was open for 0% of the time, Pallas kernels for 13%

profile of v3, /device:TPU:1, one launch (start us, length us, event | category | flops | bytes accessed | tf_op | source)
XLA Modules:
  0.0 73.3 jit_solution(15230048820900398964)
XLA Ops:
  0.6 0.0 copy-start.4
  0.6 0.0 copy-start.5
  0.7 0.0 copy-start.7
  0.7 0.0 copy-start.6
  0.7 1.5 %prompt_pack.1 = bf16[32,8,512]{2,1,0:T(8,128)(2,1)} custom-call(bf16[4,512]{1,0:T(4,128)(2,1)} %key_ref.3, bf16[4,512]{1,0:T(4,128)(2,1)} %value_ref.1), custom_call_target="tpu_custom_call" | custom-call | tf_op jit(solution)/shard_map/prompt_pack/pallas_call | solution.py:87
  2.1 14.0 %all-to-all-start = ((bf16[32,8,512]{2,1,0:T(8,128)(2,1)}), bf16[32,8,512]{2,1,0:T(8,128)(2,1)S(1)}, u32[]{:S(2)}, u32[]{:S(2)}) async-start(bf16[32,8,512]{2,1,0:T(8,128)(2,1)} %prompt_pack.1), calls=%async_computation | async-start | bytes 524288 | tf_op jit(solution)/shard_map/all_to_all | solution.py:310
  16.8 0.0 copy-start
  16.8 1.2 %copy-done = bf16[128,4096]{1,0:T(8,128)(2,1)S(1)} copy-done((bf16[128,4096]{1,0:T(8,128)(2,1)S(1)}, bf16[128,4096]{1,0:T(8,128)(2,1)}, u32[]{:S(2)}) %copy-start) | copy-done | bytes 1048600
  18.0 0.0 copy-start.1
  18.0 1.2 %copy-done.1 = bf16[128,4096]{1,0:T(8,128)(2,1)S(1)} copy-done((bf16[128,4096]{1,0:T(8,128)(2,1)S(1)}, bf16[128,4096]{1,0:T(8,128)(2,1)}, u32[]{:S(2)}) %copy-start.1) | copy-done | bytes 1048600
  19.3 0.0 copy-start.3
  19.3 0.7 copy-done.3
  19.9 1.3 %own_norms.1 = (bf16[4096,128]{1,0:T(8,128)(2,1)S(1)}, bf16[4096,128]{1,0:T(8,128)(2,1)S(1)}) custom-call(s32[1]{0:T(128)S(6)} %copy.20.len_ref, bf16[128,4096]{1,0:T(8,128)(2,1)S(1)} %copy-done, bf16[128,4096]{1,0:T(8,128)(2,1)S(1)} %copy-done.1, f32[1,128]{1,0:T(1,128)S(1)} %bitcast.7), custom_call_target="tpu_custom_call" | custom-call | flops 16777216 | bytes 4194304 | tf_op jit(solution)/shard_map/own_norms/pallas_call | solution.py:118
  21.2 7.6 %all-to-all-done.pkv_ref = bf16[32,8,512]{2,1,0:T(8,128)(2,1)S(1)} async-done(((bf16[32,8,512]{2,1,0:T(8,128)(2,1)}), bf16[32,8,512]{2,1,0:T(8,128)(2,1)S(1)}, u32[]{:S(2)}, u32[]{:S(2)}) %all-to-all-start) | async-done | bytes 262176 | tf_op jit(solution)/shard_map/all_to_all | solution.py:310
  28.8 0.0 copy-done.4
  28.8 0.0 copy-done.5
  28.8 0.0 copy-done.7
  28.8 0.0 copy-done.6
  28.8 4.6 %all_scores.1 = (bf16[4,256,1152]{2,1,0:T(8,128)(2,1)}, bf16[128,512]{1,0:T(8,128)(2,1)}, bf16[128,512]{1,0:T(8,128)(2,1)}, bf16[16,8,512]{2,1,0:T(8,128)(2,1)S(...) custom-call(s32[1]{0:T(128)} %bitcast.core_ref, bf16[4096,128]{1,0:T(8,128)(2,1)S(1)} %get-tuple-element.21.qn_ref, ...), custom_call_target="tpu_custom_call" | custom-call | flops 1073741824 | bytes 5242880 | tf_op jit(solution)/shard_map/all_scores/pallas_call | solution.py:192
  33.4 13.5 %all-to-all-start.1 = ((f32[48,2,128]{2,1,0:T(2,128)}), f32[48,2,128]{2,1,0:T(2,128)S(1)}, u32[]{:S(2)}, u32[]{:S(2)}) async-start(f32[48,2,128]{2,1,0:T(2,128)} %get-tuple-element.24), calls=%async_computation.1 | async-start | bytes 98304 | tf_op jit(solution)/shard_map/all_to_all | solution.py:310
  46.9 2.3 %collective-permute-start = (bf16[16,8,512]{2,1,0:T(8,128)(2,1)S(1)}, bf16[16,8,512]{2,1,0:T(8,128)(2,1)S(1)}, u32[]{:S(2)}, u32[]{:S(2)}) collective-permute-start(bf16[16,8,512]{2,1,0:T(8,128)(2,1)S(1)} %get-tuple-element.30), channel_id=1, source_target_pairs={{0,1},{1,0},{2,3},{3,2},{4,5},{5,4},{6,7},{7,6},{8,9},{9,8},{10,11... | collective-permute-start | bytes 393224 | tf_op jit(solution)/shard_map/ppermute | solution.py:320
  49.2 3.8 %query_back.2._ = bf16[128,4096]{1,0:T(8,128)(2,1)} custom-call(bf16[4,256,1152]{2,1,0:T(8,128)(2,1)} %get-tuple-element.23.ds_ref.a, bf16[128,4096]{1,0:T(8,128)(2,1)} %b.1, f32[1,128]{1,0:T(1,128)} %bitcast.5), custom_call_target="tpu_custom_call" | custom-call | flops 134217728 | bytes 2621440 | tf_op jit(solution)/shard_map/query_back/pallas_call | solution.py:232
  53.0 0.0 collective-permute-done.got_ref
  53.0 0.7 core_join.1.joined_hbm
  53.6 4.0 %all-to-all-done.1.arrived_ref = f32[48,2,128]{2,1,0:T(2,128)S(1)} async-done(((f32[48,2,128]{2,1,0:T(2,128)}), f32[48,2,128]{2,1,0:T(2,128)S(1)}, u32[]{:S(2)}, u32[]{:S(2)}) %all-to-all-start.1) | async-done | bytes 49184 | tf_op jit(solution)/shard_map/all_to_all | solution.py:310
  57.7 0.7 gain_relay.1
  58.4 3.6 %all-to-all-start.2 = ((bf16[16,8,640]{2,1,0:T(8,128)(2,1)}), bf16[16,8,640]{2,1,0:T(8,128)(2,1)S(1)}, u32[]{:S(2)}, u32[]{:S(2)}) async-start(bf16[16,8,640]{2,1,0:T(8,128)(2,1)} %gain_relay.1), calls=%async_computation.2 | async-start | bytes 327680 | tf_op jit(solution)/shard_map/all_to_all | solution.py:310
  62.0 0.0 copy-start.2
  62.0 3.8 %query_back.3 = bf16[128,4096]{1,0:T(8,128)(2,1)} custom-call(bf16[4,256,1152]{2,1,0:T(8,128)(2,1)} %get-tuple-element.23.ds_ref.a, bf16[128,4096]{1,0:T(8,128)(2,1)} %b.1, f32[1,128]{1,0:T(1,128)} %bitcast.6, bf16[128,4096]{1,0:T(8,128)(2,1)} %query_back.2._), custom_call_target="tpu_custom_call", output_to_operand_aliasing={{}: (3, {})} | custom-call | flops 134217728 | bytes 2621440 | tf_op jit(solution)/shard_map/query_back/pallas_call | solution.py:232
  65.8 6.8 %all-to-all-done.2.arrived_ref = bf16[16,8,640]{2,1,0:T(8,128)(2,1)S(1)} async-done(((bf16[16,8,640]{2,1,0:T(8,128)(2,1)}), bf16[16,8,640]{2,1,0:T(8,128)(2,1)S(1)}, u32[]{:S(2)}, u32[]{:S(2)}) %all-to-all-start.2) | async-done | bytes 163872 | tf_op jit(solution)/shard_map/all_to_all | solution.py:310
  72.5 0.0 copy-done.2
  72.5 0.8 %prompt_back.1 = (bf16[4,512]{1,0:T(4,128)(2,1)}, bf16[4,512]{1,0:T(4,128)(2,1)}, f32[1,128]{1,0:T(1,128)}, f32[1,128]{1,0:T(1,128)}) custom-call(bf16[16,8,640]{2,1,0:T(8,128)(2,1)S(1)} %all-to-all-done.2.arrived_ref, bf16[4,512]{1,0:T(4,128)(2,1)S(1)} %copy-done.2, f32[1,128]{1,0:T(1,128)S(1)} %bitcast.10), custom_call_target="tpu_custom_call" | custom-call | flops 1048576 | bytes 307200 | tf_op jit(solution)/shard_map/prompt_back/pallas_call | solution.py:300
Async XLA Ops:
  0.6 28.2 %copy-start.4 = (f32[128]{0:T(128)S(1)}, f32[128]{0:T(128)}, u32[]{:S(2)}) copy-start(f32[128]{0:T(128)} %param.15) | copy-start | bytes 1540
  0.6 28.2 %copy-start.5 = (f32[128]{0:T(128)S(1)}, f32[128]{0:T(128)}, u32[]{:S(2)}) copy-start(f32[128]{0:T(128)} %param.16) | copy-start | bytes 1540
  0.7 28.2 %copy-start.7 = (bf16[128,512]{1,0:T(8,128)(2,1)S(1)}, bf16[128,512]{1,0:T(8,128)(2,1)}, u32[]{:S(2)}) copy-start(bf16[128,512]{1,0:T(8,128)(2,1)} %cv_ref.1) | copy-start | bytes 393220
  0.7 28.2 %copy-start.6 = (bf16[128,512]{1,0:T(8,128)(2,1)S(1)}, bf16[128,512]{1,0:T(8,128)(2,1)}, u32[]{:S(2)}) copy-start(bf16[128,512]{1,0:T(8,128)(2,1)} %ck_ref.1) | copy-start | bytes 393220
  2.1 26.7 %all-to-all-start = ((bf16[32,8,512]{2,1,0:T(8,128)(2,1)}), bf16[32,8,512]{2,1,0:T(8,128)(2,1)S(1)}, u32[]{:S(2)}, u32[]{:S(2)}) async-start(bf16[32,8,512]{2,1,0:T(8,128)(2,1)} %prompt_pack.1), calls=%async_computation | async-start | bytes 524288 | tf_op jit(solution)/shard_map/all_to_all | solution.py:310
  16.8 1.2 %copy-start = (bf16[128,4096]{1,0:T(8,128)(2,1)S(1)}, bf16[128,4096]{1,0:T(8,128)(2,1)}, u32[]{:S(2)}) copy-start(bf16[128,4096]{1,0:T(8,128)(2,1)} %b.1) | copy-start | bytes 3145732
  18.0 1.2 %copy-start.1 = (bf16[128,4096]{1,0:T(8,128)(2,1)S(1)}, bf16[128,4096]{1,0:T(8,128)(2,1)}, u32[]{:S(2)}) copy-start(bf16[128,4096]{1,0:T(8,128)(2,1)} %do_ref.1) | copy-start | bytes 3145732
  19.3 0.7 copy-start.3
  33.4 24.3 %all-to-all-start.1 = ((f32[48,2,128]{2,1,0:T(2,128)}), f32[48,2,128]{2,1,0:T(2,128)S(1)}, u32[]{:S(2)}, u32[]{:S(2)}) async-start(f32[48,2,128]{2,1,0:T(2,128)} %get-tuple-element.24), calls=%async_computation.1 | async-start | bytes 98304 | tf_op jit(solution)/shard_map/all_to_all | solution.py:310
  46.9 6.1 %collective-permute-start = (bf16[16,8,512]{2,1,0:T(8,128)(2,1)S(1)}, bf16[16,8,512]{2,1,0:T(8,128)(2,1)S(1)}, u32[]{:S(2)}, u32[]{:S(2)}) collective-permute-start(bf16[16,8,512]{2,1,0:T(8,128)(2,1)S(1)} %get-tuple-element.30), channel_id=1, source_target_pairs={{0,1},{1,0},{2,3},{3,2},{4,5},{5,4},{6,7},{7,6},{8,9},{9,8},{10,11... | collective-permute-start | bytes 393224 | tf_op jit(solution)/shard_map/ppermute | solution.py:320
  58.4 14.2 %all-to-all-start.2 = ((bf16[16,8,640]{2,1,0:T(8,128)(2,1)}), bf16[16,8,640]{2,1,0:T(8,128)(2,1)S(1)}, u32[]{:S(2)}, u32[]{:S(2)}) async-start(bf16[16,8,640]{2,1,0:T(8,128)(2,1)} %gain_relay.1), calls=%async_computation.2 | async-start | bytes 327680 | tf_op jit(solution)/shard_map/all_to_all | solution.py:310
  62.0 10.6 %copy-start.2 = (bf16[4,512]{1,0:T(4,128)(2,1)S(1)}, bf16[4,512]{1,0:T(4,128)(2,1)}, u32[]{:S(2)}) copy-start(bf16[4,512]{1,0:T(4,128)(2,1)} %key_ref.3) | copy-start | bytes 12292
